TPU v7x, 256 devices: a whole 4x4x8 slice. The times are simulated.
256 devices in a mesh: px: 2 (over core), py: 8 (over z), ta: 16 (over y, x).
Axes of the slice: x: 4, y: 4, z: 8, core: 2. Of those that a mesh axis runs over, the one named last changes fastest.
Arguments:
- snapshots: bfloat16 [384, 5, 131072], P('ta', None, ('px', 'py')), may hold values from -6 to 6
- quad_weights: float32 [131072], P(('px', 'py')), may hold values from 1 to 10
- spectral_indices: int32 [32], replicated, may hold values from 0 to 127
Outputs:
- spectra: float32 [32, 2, 2, 5, 131072], P('ta', None, None, None, ('px', 'py'))
- gram: float32 [32, 2, 2, 2], P('ta')
All inputs are finite; a program needn't handle non-finite values.
Results may differ from a plain program's by a relative error of at most 0.0042.
Values may be sent and summed in bfloat16 or wider, within the bound.
No kernel may reach another device: no remote copies, remote signals or barrier semaphores. Data moves between devices by JAX's collectives and lax.ppermute only.
A program may use at most 128 MiB of HBM per device.

v0:
```python
import math

import jax
import jax.numpy as jnp
from jax import lax
from jax.sharding import PartitionSpec as P

VARS = 5
BLK = 256
HOP = 128
SEGMENT_NUMBER = 2
RECORD_LENGTH = 384
RETAINED_MODES = 32


def copy_for_each(shard, axis):
    devices = lax.axis_size(axis)
    return lax.all_to_all(
        jnp.broadcast_to(shard[None], (devices, *shard.shape)), axis, 0, 0, tiled=True
    )


def of_everyone(shard, axis):
    return copy_for_each(shard, axis).sum(axis=0)


def make_rotation_multipliers(spectral_indices, temporal_locations):
    segment_beginnings = jnp.arange(SEGMENT_NUMBER, dtype=jnp.int32) * HOP
    segment_shifts = temporal_locations[None, :] - segment_beginnings[:, None]
    inside = (segment_shifts >= 0) & (segment_shifts < BLK)
    window = 0.5 - 0.5 * jnp.cos(2.0 * math.pi * segment_shifts.astype(jnp.float32) / BLK)
    window = jnp.where(inside, window, jnp.float32(0.0)) / jnp.sqrt(jnp.float32(3.0 * BLK / 8.0))
    phases = jnp.mod(spectral_indices[:, None, None] * segment_shifts[None, :, :], BLK)
    angles = 2.0 * math.pi * phases.astype(jnp.float32) / BLK
    real_part = jnp.cos(angles) * window[None]
    imag_part = -jnp.sin(angles) * window[None]
    gathered_segments = jnp.stack([real_part, imag_part], axis=2)
    return gathered_segments.reshape(
        RETAINED_MODES * SEGMENT_NUMBER * 2, temporal_locations.shape[0]
    ).astype(jnp.bfloat16)


def gram_terms(spectra):
    flat = spectra.reshape(spectra.shape[0], 2 * SEGMENT_NUMBER, -1)
    inner = jnp.einsum("fam,fbm->fab", flat, flat, precision=lax.Precision.HIGHEST)
    inner = inner.reshape(spectra.shape[0], SEGMENT_NUMBER, 2, SEGMENT_NUMBER, 2)
    real_part = inner[:, :, 0, :, 0] + inner[:, :, 1, :, 1]
    imag_part = inner[:, :, 0, :, 1] - inner[:, :, 1, :, 0]
    return jnp.stack([real_part, imag_part], axis=-1)


def on_device(snapshots, quad_weights, spectral_indices):
    point_count = snapshots.shape[2]
    groups = lax.axis_size("ta")
    temporal_locations = jnp.arange(RECORD_LENGTH, dtype=jnp.int32)
    rotation_multipliers = make_rotation_multipliers(spectral_indices, temporal_locations)
    local_spectra = jnp.einsum(
        "rt,tvp->rvp",
        rotation_multipliers,
        lax.all_to_all(snapshots, "ta", split_axis=2, concat_axis=0, tiled=True),
        preferred_element_type=jnp.float32,
    )
    raw = lax.all_to_all(
        local_spectra.astype(jnp.bfloat16), "ta", split_axis=0, concat_axis=2, tiled=True
    ).astype(local_spectra.dtype)
    raw = raw.reshape(RETAINED_MODES // groups, SEGMENT_NUMBER, 2, VARS, point_count)
    spectra = raw * jnp.sqrt(quad_weights)
    summed = of_everyone(gram_terms(spectra), ("px", "py"))
    total_points = point_count * lax.axis_size("px") * lax.axis_size("py")
    gram = summed / jnp.float32(total_points * VARS)
    return (spectra, gram)


def solution(mesh):
    return jax.shard_map(
        on_device,
        mesh=mesh,
        in_specs=(P("ta", None, ("px", "py")), P(("px", "py")), P()),
        out_specs=(P("ta", None, None, None, ("px", "py")), P("ta", None, None, None)),
        check_vma=False,
    )
```

profile of v0, /device:TPU:1, one launch (start us, length us, event | category | flops | bytes accessed | tf_op | source)
XLA Modules:
  0.0 153.8 jit_solution(5036630691097740982)
XLA Ops:
  0.6 14.4 %copy.48 = bf16[24,5,8192]{0,1,2:T(8,128)(2,1)} copy(bf16[24,5,8192]{2,0,1:T(8,128)(2,1)} %param.3) | data formatting | bytes 3932160 | tf_op args[0]
  15.0 19.3 %reshape.183 = bf16[16,2,30720]{2,1,0:T(2,128)(2,1)} reshape(bf16[8192,5,24]{2,1,0:T(8,128)(2,1)} %bitcast.24) | data formatting | bytes 3932160
  34.4 7.7 %all-to-all-start = ((bf16[16,2,30720]{2,1,0:T(2,128)(2,1)}), bf16[16,2,30720]{2,1,0:T(2,128)(2,1)S(1)}, u32[]{:S(2)}, u32[]{:S(2)}) async-start(bf16[16,2,30720]{2,1,0:T(2,128)(2,1)} %reshape.183), calls=%async_computation | async-start | bytes 3932160 | tf_op jit(solution)/shard_map/all_to_all | solution.py:60
  42.3 0.5 multiply_convert_fusion.1
  43.0 28.0 %all-to-all-done = bf16[16,2,30720]{2,1,0:T(2,128)(2,1)S(1)} async-done(((bf16[16,2,30720]{2,1,0:T(2,128)(2,1)}), bf16[16,2,30720]{2,1,0:T(2,128)(2,1)S(1)}, u32[]{:S(2)}, u32[]{:S(2)}) %all-to-all-start) | async-done | bytes 1966112 | tf_op jit(solution)/shard_map/all_to_all | solution.py:60
  70.9 15.5 %reshape.184 = bf16[8192,5,24]{2,1,0:T(8,128)(2,1)} reshape(bf16[16,2,30720]{2,1,0:T(2,128)(2,1)S(1)} %all-to-all-done) | data formatting | bytes 3932160
  86.4 14.6 %copy.49 = bf16[24,5,16,512]{3,0,2,1:T(8,128)(2,1)S(1)} copy(bf16[24,5,16,512]{0,1,3,2:T(8,128)(2,1)} %bitcast.23) | data formatting | bytes 3932160 | tf_op jit(solution)/shard_map/all_to_all | solution.py:60
  101.0 0.5 convolution_convert_fusion
  101.5 1.3 copy.50
  102.8 4.3 %all-to-all-start.1 = ((bf16[128,5,512]{2,1,0:T(8,128)(2,1)}), bf16[128,5,512]{2,1,0:T(8,128)(2,1)S(1)}, u32[]{:S(2)}, u32[]{:S(2)}) async-start(bf16[128,5,512]{2,1,0:T(8,128)(2,1)} %copy.50), calls=%async_computation.1 | async-start | bytes 2097152 | tf_op jit(solution)/shard_map/all_to_all | solution.py:63
  107.2 0.7 mul.107
  108.0 14.7 %all-to-all-done.1 = bf16[128,5,512]{2,1,0:T(8,128)(2,1)S(1)} async-done(((bf16[128,5,512]{2,1,0:T(8,128)(2,1)}), bf16[128,5,512]{2,1,0:T(8,128)(2,1)S(1)}, u32[]{:S(2)}, u32[]{:S(2)}) %all-to-all-start.1) | async-done | bytes 655392 | tf_op jit(solution)/shard_map/all_to_all | solution.py:63
  122.7 1.5 copy.59
  124.2 0.3 convert_bitcast_fusion
  124.5 2.2 %reshape.176 = f32[2,4,40960]{2,1,0:T(4,128)S(1)} reshape(f32[8,5,16,512]{3,2,1,0:T(8,128)} %bitcast.28) | data formatting | bytes 2621440 | tf_op jit(solution)/shard_map/convert_element_type | solution.py:65
  126.7 6.8 %fusion = f32[2,4,4]{2,1,0:T(4,128)S(1)} fusion(f32[2,4,40960]{2,1,0:T(4,128)S(1)} %reshape.176, f32[40960]{0:T(1024)} %mul.107), kind=kOutput, calls=%fused_computation.2 | convolution fusion | flops 16056320 | bytes 1474688 | tf_op jit(solution)/shard_map/fam,fbm->fab/dot_general | solution.py:45
  133.9 0.6 broadcast_in_dim.7
  134.6 11.5 %all-to-all-start.2 = ((f32[16,2,2,2,2]{4,3,2,1,0:T(2,128)}), f32[16,2,2,2,2]{4,3,2,1,0:T(2,128)S(1)}, u32[]{:S(2)}, u32[]{:S(2)}) async-start(f32[16,2,2,2,2]{4,3,2,1,0:T(2,128)} %broadcast_in_dim.7), calls=%async_computation.2 | async-start | bytes 131072 | tf_op jit(solution)/shard_map/all_to_all | solution.py:18
  146.0 0.8 copy.52
  146.8 1.1 reshape.175
  147.9 0.5 broadcast_multiply_fusion
  148.5 1.1 copy.55
  149.6 3.5 %all-to-all-done.2 = f32[16,2,2,2,2]{4,3,2,1,0:T(2,128)S(1)} async-done(((f32[16,2,2,2,2]{4,3,2,1,0:T(2,128)}), f32[16,2,2,2,2]{4,3,2,1,0:T(2,128)S(1)}, u32[]{:S(2)}, u32[]{:S(2)}) %all-to-all-start.2) | async-done | bytes 1056 | tf_op jit(solution)/shard_map/all_to_all | solution.py:18
  153.2 0.6 broadcast_multiply_fusion.1
  (17 shorter events, 0.8 us)
Async XLA Ops:
  34.4 7.9 %copy-start.1 = (s32[32]{0:T(128)S(1)}, s32[32]{0:T(128)}, u32[]{:S(2)}) copy-start(s32[32]{0:T(128)} %param.5) | copy-start | bytes 388
  34.4 36.5 %all-to-all-start = ((bf16[16,2,30720]{2,1,0:T(2,128)(2,1)}), bf16[16,2,30720]{2,1,0:T(2,128)(2,1)S(1)}, u32[]{:S(2)}, u32[]{:S(2)}) async-start(bf16[16,2,30720]{2,1,0:T(2,128)(2,1)} %reshape.183), calls=%async_computation | async-start | bytes 3932160 | tf_op jit(solution)/shard_map/all_to_all | solution.py:60
  102.8 4.3 %copy-start = (f32[8192]{0:T(1024)S(1)}, f32[8192]{0:T(1024)}, u32[]{:S(2)}) copy-start(f32[8192]{0:T(1024)} %param.4) | copy-start | bytes 98308
  102.8 19.9 %all-to-all-start.1 = ((bf16[128,5,512]{2,1,0:T(8,128)(2,1)}), bf16[128,5,512]{2,1,0:T(8,128)(2,1)S(1)}, u32[]{:S(2)}, u32[]{:S(2)}) async-start(bf16[128,5,512]{2,1,0:T(8,128)(2,1)} %copy.50), calls=%async_computation.1 | async-start | bytes 2097152 | tf_op jit(solution)/shard_map/all_to_all | solution.py:63
  134.6 18.6 %all-to-all-start.2 = ((f32[16,2,2,2,2]{4,3,2,1,0:T(2,128)}), f32[16,2,2,2,2]{4,3,2,1,0:T(2,128)S(1)}, u32[]{:S(2)}, u32[]{:S(2)}) async-start(f32[16,2,2,2,2]{4,3,2,1,0:T(2,128)} %broadcast_in_dim.7), calls=%async_computation.2 | async-start | bytes 131072 | tf_op jit(solution)/shard_map/all_to_all | solution.py:18
where the time goes:
time: 155 us; the launch traced here: 154 us
  local copies, waits for them, and re-layouts  73.6 us (47%)
  waiting for transfers between devices  46.2 us (30%)
  starting transfers between devices  23.5 us (15%)
  matrix products  7.34 us (5%)
  other arithmetic  2.34 us (2%)
    unnamed x8, local copies, waits for them, and re-layouts  50.4 us
    all_to_all x1, waiting for transfers between devices, on_device(): lax.all_to_all(snapshots, 'ta', split_axis=2, concat_axis=0, tiled=True)  28 us
    all_to_all x1, waiting for transfers between devices, on_device(): lax.all_to_all(local_spectra.astype(jnp.bfloat16), 'ta', split_axis=0, co...  14.7 us
    all_to_all x1, local copies, waits for them, and re-layouts, on_device(): lax.all_to_all(snapshots, 'ta', split_axis=2, concat_axis=0, tiled=True)  14.6 us
    all_to_all x1, starting transfers between devices, copy_for_each(): lax.all_to_all(jnp.broadcast_to(shard[None], (devices, *shard.shape)), ax...  11.5 us
    all_to_all x1, starting transfers between devices, on_device(): lax.all_to_all(snapshots, 'ta', split_axis=2, concat_axis=0, tiled=True)  7.7 us
    dot_general x1, matrix products, gram_terms(): jnp.einsum('fam,fbm->fab', flat, flat, precision=lax.Precision.HIGHEST)  6.84 us
    convert_element_type x4, local copies, waits for them, and re-layouts, on_device(): raw = lax.all_to_all(local_spectra.astype(jnp.bfloat16), 'ta', split_axis...  5.6 us
  transfers between devices with their start and end apart: 3, of which 3 were waited for; matrix products, arithmetic and copies ran while one was open for 3% of the time, Pallas kernels for 0%

commit v1 on v0

v1 whole, which is shorter than its diff:
```python
import math

import jax
import jax.numpy as jnp
from jax import lax
from jax.experimental import pallas as pl
from jax.experimental.pallas import tpu as pltpu
from jax.sharding import PartitionSpec as P

VARS = 5
BLK = 256
HOP = 128
SEGMENT_NUMBER = 2
RECORD_LENGTH = 384
RETAINED_MODES = 32
LANES = 128


def make_rotation_multipliers(spectral_indices, temporal_locations):
    segment_beginnings = jnp.arange(SEGMENT_NUMBER, dtype=jnp.int32) * HOP
    segment_shifts = temporal_locations[None, :] - segment_beginnings[:, None]
    inside = (segment_shifts >= 0) & (segment_shifts < BLK)
    window = 0.5 - 0.5 * jnp.cos(2.0 * math.pi * segment_shifts.astype(jnp.float32) / BLK)
    window = jnp.where(inside, window, jnp.float32(0.0)) / jnp.sqrt(jnp.float32(3.0 * BLK / 8.0))
    phases = jnp.mod(spectral_indices[None, :, None] * segment_shifts[:, None, :], BLK)
    angles = 2.0 * math.pi * phases.astype(jnp.float32) / BLK
    real_part = jnp.cos(angles) * window[:, None]
    imag_part = -jnp.sin(angles) * window[:, None]
    return (
        jnp.stack([real_part, imag_part], axis=0)
        .reshape(2 * SEGMENT_NUMBER * RETAINED_MODES, temporal_locations.shape[0])
        .astype(jnp.bfloat16)
    )


def pack(shard, groups):
    variables, times, points = shard.shape
    piece = points // groups
    per_step = 4

    def body(x_ref, o_ref):
        for d in range(per_step):
            o_ref[d] = x_ref[:, :, d * piece : (d + 1) * piece]

    return pl.pallas_call(
        body,
        grid=(groups // per_step,),
        in_specs=[pl.BlockSpec((variables, times, per_step * piece), lambda j: (0, 0, j))],
        out_specs=pl.BlockSpec((per_step, variables, times, piece), lambda j: (j, 0, 0, 0)),
        out_shape=jax.ShapeDtypeStruct((groups, variables, times, piece), shard.dtype),
        name="pack",
    )(shard)


def transform(gathered, multipliers, weights, group):
    groups, variables, times, piece = gathered.shape
    rows = multipliers.shape[0]
    tiles = piece // LANES
    modes = RETAINED_MODES
    per_mode = SEGMENT_NUMBER * variables * tiles * 2

    def body(g_ref, x_ref, m_ref, w_ref, z_ref, gram_ref, f_ref, acc_ref):
        m = m_ref[...]
        acc_ref[...] = jnp.zeros_like(acc_ref)
        sw = jnp.sqrt(w_ref[pl.ds(g_ref[0] * tiles, tiles), :])
        for v in range(variables):
            x = x_ref[:, v].reshape(groups * times, piece)
            s = jnp.dot(m, x, preferred_element_type=jnp.float32)
            for j in range(tiles):
                q = s[:, j * LANES : (j + 1) * LANES] * sw[j : j + 1, :]
                parts = {}
                for c in range(2):
                    for b in range(SEGMENT_NUMBER):
                        at = (c * SEGMENT_NUMBER + b) * modes
                        part = q[at : at + modes]
                        parts[c, b] = part
                        first = (b * variables + v) * tiles * 2 + j * 2 + c
                        f_ref[pl.ds(first, modes, stride=per_mode), :] = part
                r0, r1, i0, i1 = parts[0, 0], parts[0, 1], parts[1, 0], parts[1, 1]
                acc_ref[0:modes] += r0 * r0 + i0 * i0
                acc_ref[modes : 2 * modes] += r1 * r1 + i1 * i1
                acc_ref[2 * modes : 3 * modes] += r0 * r1 + i0 * i1
                acc_ref[3 * modes : 4 * modes] += r0 * i1 - i0 * r1
        z_ref[...] = f_ref[...].astype(z_ref.dtype)
        gram_ref[...] = lax.dot_general(
            jnp.ones((8, LANES), jnp.float32),
            acc_ref[...],
            (((1,), (1,)), ((), ())),
            precision=lax.Precision.HIGHEST,
            preferred_element_type=jnp.float32,
        )

    vmem = pl.BlockSpec(memory_space=pltpu.VMEM)
    return pl.pallas_call(
        body,
        in_specs=[pl.BlockSpec(memory_space=pltpu.SMEM), vmem, vmem, vmem],
        out_specs=(vmem, vmem),
        out_shape=(
            jax.ShapeDtypeStruct((modes * per_mode, LANES), jnp.bfloat16),
            jax.ShapeDtypeStruct((8, LANES), jnp.float32),
        ),
        scratch_shapes=[
            pltpu.VMEM((modes * per_mode, LANES), jnp.float32),
            pltpu.VMEM((4 * modes, LANES), jnp.float32),
        ],
        name="transform",
    )(group, gathered, multipliers, weights)


def unpack(received, groups):
    _, outer, inner, lanes = received.shape
    per_step = 5

    def body(y_ref, o_ref):
        for s in range(groups):
            o_ref[:, s * inner : (s + 1) * inner, :] = y_ref[s].astype(jnp.float32)

    return pl.pallas_call(
        body,
        grid=(outer // per_step,),
        in_specs=[pl.BlockSpec((groups, per_step, inner, lanes), lambda k: (0, k, 0, 0))],
        out_specs=pl.BlockSpec((per_step, groups * inner, lanes), lambda k: (k, 0, 0)),
        out_shape=jax.ShapeDtypeStruct((outer, groups * inner, lanes), jnp.float32),
        name="unpack",
    )(received)


def on_device(snapshots, quad_weights, spectral_indices):
    point_count = snapshots.shape[2]
    groups = lax.axis_size("ta")
    me = lax.axis_index("ta")
    own = RETAINED_MODES // groups
    piece = point_count // groups
    tiles = piece // LANES
    temporal_locations = jnp.arange(RECORD_LENGTH, dtype=jnp.int32)
    multipliers = make_rotation_multipliers(spectral_indices, temporal_locations)

    packed = pack(jnp.transpose(snapshots, (1, 0, 2)), groups)
    gathered = lax.all_to_all(packed, "ta", split_axis=0, concat_axis=0, tiled=True)
    weights = quad_weights.reshape(point_count // LANES, LANES)
    payload, partial = transform(gathered, multipliers, weights, me[None].astype(jnp.int32))
    payload = payload.reshape(groups, own * SEGMENT_NUMBER * VARS, tiles * 2, LANES)
    received = lax.all_to_all(payload, "ta", split_axis=0, concat_axis=0, tiled=True)

    summed = lax.psum(partial, ("px", "py", "ta"))
    total_points = point_count * lax.axis_size("px") * lax.axis_size("py")
    terms = lax.dynamic_slice_in_dim(summed[0].reshape(4, RETAINED_MODES), me * own, own, axis=1)
    terms = terms / jnp.float32(total_points * VARS)
    p00, p11, real, imag = terms[0], terms[1], terms[2], terms[3]
    zero = jnp.zeros_like(p00)
    gram = jnp.stack([p00, zero, real, imag, real, -imag, p11, zero], axis=-1)
    gram = gram.reshape(own, SEGMENT_NUMBER, SEGMENT_NUMBER, 2)

    spectra = unpack(received, groups)
    spectra = spectra.reshape(own, SEGMENT_NUMBER, VARS, point_count // LANES, 2, LANES)
    spectra = jnp.transpose(spectra, (0, 1, 4, 2, 3, 5)).reshape(own, SEGMENT_NUMBER, 2, VARS, point_count)
    return (spectra, gram)


def solution(mesh):
    return jax.shard_map(
        on_device,
        mesh=mesh,
        in_specs=(P("ta", None, ("px", "py")), P(("px", "py")), P()),
        out_specs=(P("ta", None, None, None, ("px", "py")), P("ta", None, None, None)),
        check_vma=False,
    )
```

time: 155 us -> 137 us (0.88)
  blocking collectives: 0 us -> 81 us
  local copies, waits for them, and re-layouts: 73.6 us -> 3.5 us
  waiting for transfers between devices: 46.2 us -> 27.5 us
  starting transfers between devices: 23.5 us -> 11.9 us
  Pallas kernels: 0 us -> 10.4 us
  matrix products: 7.34 us -> 0 us
    psum x0 -> x1, blocking collectives: none -> 81 us  [on_device(): summed = lax.psum(partial, ('px', 'py', 'ta'))]
    unnamed x8 -> x6, local copies, waits for them, and re-layouts: 50.4 us -> 2.14 us
    all_to_all x3 -> x2, waiting for transfers between devices: 46.2 us -> 27.5 us  [the longest x1 27.5 us: on_device(): lax.all_to_all(packed, 'ta', split_axis=0, concat_axis=0, tiled=True)]
    all_to_all x1 -> x0, local copies, waits for them, and re-layouts: 14.6 us -> none  [on_device(): lax.all_to_all(snapshots, 'ta', split_axis=2, concat_axis=0, tiled=True)]
    all_to_all x3 -> x2, starting transfers between devices: 23.5 us -> 11.9 us  [the longest x1 7.7 us: on_device(): lax.all_to_all(packed, 'ta', split_axis=0, concat_axis=0, tiled=True)]
    pallas_call x0 -> x3, Pallas kernels: none -> 10.4 us  [the longest x1 3.74 us: pack(): pl.pallas_call(body, grid=(groups // per_step,), in_specs=[pl.BlockSpec((...]
    dot_general x2 -> x0, matrix products: 7.34 us -> none  [the longest x1 6.84 us: gram_terms(): jnp.einsum('fam,fbm->fab', flat, flat, precision=lax.Precision.HIGHEST)]
    convert_element_type x6 -> x0, local copies, waits for them, and re-layouts: 6.99 us -> none  [the longest x4 5.6 us: on_device(): raw = lax.all_to_all(local_spectra.astype(jnp.bfloat16), 'ta', split_axis...]
  transfers between devices with their start and end apart: 3 -> 2, of which waited for: 3 -> 1; matrix products, arithmetic and copies ran while one was open for 3% -> 2% of each run, Pallas kernels for 0% -> 0%
where the time goes in v1:
time: 137 us; the launch traced here: 136 us
  blocking collectives  81 us (59%)
  waiting for transfers between devices  27.5 us (20%)
  starting transfers between devices  11.9 us (9%)
  Pallas kernels  10.4 us (8%)
  local copies, waits for them, and re-layouts  3.5 us (3%)
  other arithmetic  1.42 us (1%)
    psum x1, blocking collectives, on_device(): summed = lax.psum(partial, ('px', 'py', 'ta'))  81 us
    all_to_all x1, waiting for transfers between devices, on_device(): lax.all_to_all(packed, 'ta', split_axis=0, concat_axis=0, tiled=True)  27.5 us
    all_to_all x1, starting transfers between devices, on_device(): lax.all_to_all(packed, 'ta', split_axis=0, concat_axis=0, tiled=True)  7.7 us
    all_to_all x1, starting transfers between devices, on_device(): lax.all_to_all(payload, 'ta', split_axis=0, concat_axis=0, tiled=True)  4.2 us
    pallas_call x1, Pallas kernels, pack(): pl.pallas_call(body, grid=(groups // per_step,), in_specs=[pl.BlockSpec((...  3.74 us
    pallas_call x1, Pallas kernels, unpack(): pl.pallas_call(body, grid=(outer // per_step,), in_specs=[pl.BlockSpec((g...  3.35 us
    pallas_call x1, Pallas kernels, transform(): pl.pallas_call(body, in_specs=[pl.BlockSpec(memory_space=pltpu.SMEM), vme...  3.31 us
  transfers between devices with their start and end apart: 2, of which 1 were waited for; matrix products, arithmetic and copies ran while one was open for 2% of the time, Pallas kernels for 0%

profile of v1, /device:TPU:1, one launch (start us, length us, event | category | flops | bytes accessed | tf_op | source)
XLA Modules:
  0.0 136.4 jit_solution(14290359459364511540)
XLA Ops:
  0.6 3.7 %pack.1 = bf16[16,5,24,512]{3,2,1,0:T(8,128)(2,1)} custom-call(bf16[5,24,8192]{2,1,0:T(8,128)(2,1)} %bitcast.20), custom_call_target="tpu_custom_call" | custom-call | tf_op jit(solution)/shard_map/pack/pallas_call | solution.py:45
  4.4 7.7 %all-to-all-start = ((bf16[16,5,24,512]{3,2,1,0:T(8,128)(2,1)}), bf16[16,5,24,512]{3,2,1,0:T(8,128)(2,1)S(1)}, u32[]{:S(2)}, u32[]{:S(2)}) async-start(bf16[16,5,24,512]{3,2,1,0:T(8,128)(2,1)} %pack.1), calls=%async_computation | async-start | bytes 3932160 | tf_op jit(solution)/shard_map/all_to_all | solution.py:139
  12.1 0.1 fusion.3
  12.2 0.1 iota_subtract_fusion
  12.3 0.0 copy-done.2
  12.3 0.5 multiply_convert_fusion.1
  12.8 0.7 pad_maximum_fusion
  13.4 27.5 %all-to-all-done.x_ref = bf16[16,5,24,512]{3,2,1,0:T(8,128)(2,1)S(1)} async-done(((bf16[16,5,24,512]{3,2,1,0:T(8,128)(2,1)}), bf16[16,5,24,512]{3,2,1,0:T(8,128)(2,1)S(1)}, u32[]{:S(2)}, u32[]{:S(2)}) %all-to-all-start) | async-done | bytes 1966112 | tf_op jit(solution)/shard_map/all_to_all | solution.py:139
  40.9 1.3 copy-done
  42.2 3.3 %transform.1 = (bf16[2560,128]{1,0:T(8,128)(2,1)}, f32[8,128]{1,0:T(8,128)}) custom-call(s32[1]{0:T(128)} %bitcast.g_ref, bf16[16,5,24,512]{3,2,1,0:T(8,128)(2,1)} %copy-done, bf16[128,384]{1,0:T(8,128)(2,1)} %bitcast.23, f32[64,128]{1,0:T(8,128)} %bitcast.24), custom_call_target="tpu_custom_call" | custom-call | tf_op jit(solution)/shard_map/transform/pallas_call | solution.py:94
  45.5 4.2 %all-to-all-start.1 = ((bf16[16,20,8,128]{3,2,1,0:T(8,128)(2,1)}), bf16[16,20,8,128]{3,2,1,0:T(8,128)(2,1)S(1)}, u32[]{:S(2)}, u32[]{:S(2)}) async-start(bf16[16,20,8,128]{3,2,1,0:T(8,128)(2,1)} %bitcast.22), calls=%async_computation.1 | async-start | bytes 1310720 | tf_op jit(solution)/shard_map/all_to_all | solution.py:143
  49.7 81.0 %psum.7 = f32[8,128]{1,0:T(8,128)S(1)} all-reduce(f32[8,128]{1,0:T(8,128)} %get-tuple-element.5), channel_id=1, replica_groups=mesh['px'=2,'py'=8,'ta'=16] {'px','py','ta'}, use_global_device_ids=true, to_apply=%region_0.1 | all-reduce | flops 1024 | bytes 8192 | tf_op jit(solution)/shard_map/psum | solution.py:145
  130.8 0.1 reshape_squeeze.3
  130.9 0.1 dynamic-slice_multiply_fusion
  131.0 0.1 copy.8
  131.0 0.1 copy.9
  131.1 0.1 copy.10
  131.2 0.1 copy.12
  131.3 0.1 copy.13
  131.4 0.1 stack.11
  131.5 0.7 reshape.139
  132.2 0.0 all-to-all-done.1.y_ref
  132.2 0.8 copy-done.1
  133.1 3.3 %unpack.1 = f32[20,128,128]{2,1,0:T(8,128)} custom-call(bf16[16,20,8,128]{3,2,1,0:T(8,128)(2,1)} %copy-done.1), custom_call_target="tpu_custom_call" | custom-call | tf_op jit(solution)/shard_map/unpack/pallas_call | solution.py:118
  (8 shorter events, 0.0 us)
Async XLA Ops:
  4.4 7.9 %copy-start.2 = (s32[32]{0:T(128)S(1)}, s32[32]{0:T(128)}, u32[]{:S(2)}) copy-start(s32[32]{0:T(128)} %param.5) | copy-start | bytes 388
  4.4 36.5 %all-to-all-start = ((bf16[16,5,24,512]{3,2,1,0:T(8,128)(2,1)}), bf16[16,5,24,512]{3,2,1,0:T(8,128)(2,1)S(1)}, u32[]{:S(2)}, u32[]{:S(2)}) async-start(bf16[16,5,24,512]{3,2,1,0:T(8,128)(2,1)} %pack.1), calls=%async_computation | async-start | bytes 3932160 | tf_op jit(solution)/shard_map/all_to_all | solution.py:139
  40.9 1.3 copy-start
  45.5 86.7 %all-to-all-start.1 = ((bf16[16,20,8,128]{3,2,1,0:T(8,128)(2,1)}), bf16[16,20,8,128]{3,2,1,0:T(8,128)(2,1)S(1)}, u32[]{:S(2)}, u32[]{:S(2)}) async-start(bf16[16,20,8,128]{3,2,1,0:T(8,128)(2,1)} %bitcast.22), calls=%async_computation.1 | async-start | bytes 1310720 | tf_op jit(solution)/shard_map/all_to_all | solution.py:143
  132.2 0.8 copy-start.1

commit v2 on v1

v2 whole, which is shorter than its diff:
```python
import math

import jax
import jax.numpy as jnp
from jax import lax
from jax.experimental import pallas as pl
from jax.experimental.pallas import tpu as pltpu
from jax.sharding import PartitionSpec as P


VARS = 5
BLK = 256
HOP = 128
SEGMENT_NUMBER = 2
RECORD_LENGTH = 384
RETAINED_MODES = 32
LANES = 128
VMEM_LIMIT = 16 << 20
EXTRA = 8


def make_rotation_multipliers(spectral_indices, temporal_locations):
    segment_beginnings = jnp.arange(SEGMENT_NUMBER, dtype=jnp.int32) * HOP
    segment_shifts = temporal_locations[None, :] - segment_beginnings[:, None]
    inside = (segment_shifts >= 0) & (segment_shifts < BLK)
    window = 0.5 - 0.5 * jnp.cos(2.0 * math.pi * segment_shifts.astype(jnp.float32) / BLK)
    window = jnp.where(inside, window, jnp.float32(0.0)) / jnp.sqrt(jnp.float32(3.0 * BLK / 8.0))
    phases = jnp.mod(spectral_indices[None, :, None] * segment_shifts[:, None, :], BLK)
    angles = 2.0 * math.pi * phases.astype(jnp.float32) / BLK
    real_part = jnp.cos(angles) * window[:, None]
    imag_part = -jnp.sin(angles) * window[:, None]
    return (
        jnp.stack([real_part, imag_part], axis=0)
        .reshape(2 * SEGMENT_NUMBER * RETAINED_MODES, temporal_locations.shape[0])
        .astype(jnp.bfloat16)
    )


def pack(shard, groups):
    variables, times, points = shard.shape
    piece = points // groups

    def body(x_ref, o_ref, held, in_sem, out_sem):
        def take(d):
            return pltpu.make_async_copy(x_ref.at[:, :, pl.ds(d * piece, piece)], held.at[d], in_sem.at[d])

        def put(d):
            return pltpu.make_async_copy(held.at[d], o_ref.at[d], out_sem.at[d])

        for d in range(groups):
            take(d).start()
        for d in range(groups):
            take(d).wait()
            put(d).start()
        for d in range(groups):
            put(d).wait()

    shape = (groups, variables, times, piece)
    return pl.pallas_call(
        body,
        in_specs=[pl.BlockSpec(memory_space=pltpu.HBM)],
        out_specs=pl.BlockSpec(memory_space=pltpu.HBM),
        out_shape=jax.ShapeDtypeStruct(shape, shard.dtype),
        scratch_shapes=[
            pltpu.VMEM(shape, shard.dtype),
            pltpu.SemaphoreType.DMA((groups,)),
            pltpu.SemaphoreType.DMA((groups,)),
        ],
        name="pack",
    )(shard)


def transform(gathered, multipliers, weights, group):
    groups, variables, times, piece = gathered.shape
    tiles = piece // LANES
    modes = RETAINED_MODES
    own = modes // groups
    per_mode = SEGMENT_NUMBER * variables * tiles * 2
    height = own * per_mode + EXTRA

    def body(g_ref, x_ref, m_ref, w_ref, z_ref, f_ref, acc_ref):
        m = m_ref[...]
        acc_ref[...] = jnp.zeros_like(acc_ref)
        sw = jnp.sqrt(w_ref[pl.ds(g_ref[0] * tiles, tiles), :])
        for v in range(variables):
            x = x_ref[:, v].reshape(groups * times, piece)
            s = jnp.dot(m, x, preferred_element_type=jnp.float32)
            for j in range(tiles):
                q = s[:, j * LANES : (j + 1) * LANES] * sw[j : j + 1, :]
                parts = {}
                for c in range(2):
                    for b in range(SEGMENT_NUMBER):
                        at = (c * SEGMENT_NUMBER + b) * modes
                        part = q[at : at + modes]
                        parts[c, b] = part
                        for k in range(own):
                            first = k * per_mode + (b * variables + v) * tiles * 2 + j * 2 + c
                            f_ref[pl.ds(first, groups, stride=height), :] = part[k * groups : (k + 1) * groups]
                r0, r1, i0, i1 = parts[0, 0], parts[0, 1], parts[1, 0], parts[1, 1]
                acc_ref[0:modes] += r0 * r0 + i0 * i0
                acc_ref[modes : 2 * modes] += r1 * r1 + i1 * i1
                acc_ref[2 * modes : 3 * modes] += r0 * r1 + i0 * i1
                acc_ref[3 * modes : 4 * modes] += r0 * i1 - i0 * r1
        total = lax.dot_general(
            jnp.ones((EXTRA, LANES), jnp.float32),
            acc_ref[...],
            (((1,), (1,)), ((), ())),
            precision=lax.Precision.HIGHEST,
            preferred_element_type=jnp.float32,
        )
        rounded = total.astype(jnp.bfloat16).astype(jnp.float32)
        row = lax.broadcasted_iota(jnp.int32, total.shape, 0)
        tail = jnp.where(row == 0, rounded, jnp.where(row == 1, total - rounded, 0.0))
        for d in range(groups):
            f_ref[d * height + own * per_mode : (d + 1) * height, :] = tail
        z_ref[...] = f_ref[...].astype(z_ref.dtype)

    vmem = pl.BlockSpec(memory_space=pltpu.VMEM)
    return pl.pallas_call(
        body,
        in_specs=[pl.BlockSpec(memory_space=pltpu.SMEM), vmem, vmem, vmem],
        out_specs=vmem,
        out_shape=jax.ShapeDtypeStruct((groups * height, LANES), jnp.bfloat16),
        scratch_shapes=[
            pltpu.VMEM((groups * height, LANES), jnp.float32),
            pltpu.VMEM((4 * modes, LANES), jnp.float32),
        ],
        compiler_params=pltpu.CompilerParams(vmem_limit_bytes=VMEM_LIMIT),
        name="transform",
    )(group, gathered, multipliers, weights).reshape(groups, height, LANES)


def unpack(received, rows, inner):
    groups, _, lanes = received.shape
    outer = rows // inner
    per_step = 5

    def body(y_ref, o_ref):
        for s in range(groups):
            o_ref[:, s * inner : (s + 1) * inner, :] = y_ref[s].astype(jnp.float32).reshape(per_step, inner, lanes)

    return pl.pallas_call(
        body,
        grid=(outer // per_step,),
        in_specs=[pl.BlockSpec((groups, per_step * inner, lanes), lambda k: (0, k, 0))],
        out_specs=pl.BlockSpec((per_step, groups * inner, lanes), lambda k: (k, 0, 0)),
        out_shape=jax.ShapeDtypeStruct((outer, groups * inner, lanes), jnp.float32),
        compiler_params=pltpu.CompilerParams(vmem_limit_bytes=VMEM_LIMIT),
        name="unpack",
    )(received)


def gram_choice(me, own, terms):
    shape = (own, SEGMENT_NUMBER, SEGMENT_NUMBER, 2, LANES)
    f, b, b2, part, lane = (lax.broadcasted_iota(jnp.int32, shape, d) for d in range(5))
    q = jnp.where(b == b2, b, 2 + part)
    sign = jnp.where(part == 0, 1.0, (b2 - b).astype(jnp.float32))
    return jnp.where(lane == q * RETAINED_MODES + f * (RETAINED_MODES // own) + me, sign / jnp.float32(terms), 0.0)


def on_device(snapshots, quad_weights, spectral_indices):
    point_count = snapshots.shape[2]
    groups = lax.axis_size("ta")
    me = lax.axis_index("ta")
    own = RETAINED_MODES // groups
    piece = point_count // groups
    tiles = piece // LANES
    split = ("px", "py")
    copies = lax.axis_size(split)
    temporal_locations = jnp.arange(RECORD_LENGTH, dtype=jnp.int32)
    by_place = spectral_indices.reshape(groups, own).T.reshape(RETAINED_MODES)
    multipliers = make_rotation_multipliers(by_place, temporal_locations)

    packed = pack(jnp.transpose(snapshots, (1, 0, 2)), groups)
    gathered = lax.all_to_all(packed, "ta", split_axis=0, concat_axis=0, tiled=True)
    weights = quad_weights.reshape(point_count // LANES, LANES)
    payload = transform(gathered, multipliers, weights, me[None].astype(jnp.int32))
    received = lax.all_to_all(payload, "ta", split_axis=0, concat_axis=0, tiled=True)

    rows = own * SEGMENT_NUMBER * VARS * tiles * 2
    partial = jnp.sum(received[:, rows : rows + 2].astype(jnp.float32), axis=(0, 1))
    partial = jnp.broadcast_to(partial[None, None], (copies, 1, LANES))
    partial = lax.all_to_all(partial, split, split_axis=0, concat_axis=0, tiled=True)
    choice = gram_choice(me, own, point_count * copies * VARS)
    gram = jnp.sum(choice * jnp.sum(partial, axis=(0, 1)), axis=-1)

    spectra = unpack(received, rows, tiles * 2)
    spectra = spectra.reshape(own, SEGMENT_NUMBER, VARS, point_count // LANES, 2, LANES)
    spectra = jnp.transpose(spectra, (0, 1, 4, 2, 3, 5)).reshape(own, SEGMENT_NUMBER, 2, VARS, point_count)
    return (spectra, gram)


def solution(mesh):
    return jax.shard_map(
        on_device,
        mesh=mesh,
        in_specs=(P("ta", None, ("px", "py")), P(("px", "py")), P()),
        out_specs=(P("ta", None, None, None, ("px", "py")), P("ta", None, None, None)),
        check_vma=False,
    )
```

time: 137 us -> 77 us (0.56)
  blocking collectives: 81 us -> 0 us
  waiting for transfers between devices: 27.5 us -> 44.8 us
  starting transfers between devices: 11.9 us -> 22.6 us
  Pallas kernels: 10.4 us -> 6.16 us
  local copies, waits for them, and re-layouts: 3.5 us -> 0.86 us
    psum x1 -> x0, blocking collectives: 81 us -> none  [on_device(): summed = lax.psum(partial, ('px', 'py', 'ta'))]
    all_to_all x1, waiting for transfers between devices: 0.01 us -> 11.9 us  [on_device(): lax.all_to_all(payload, 'ta', split_axis=0, concat_axis=0, tiled=True)]
    all_to_all x0 -> x1, starting transfers between devices: none -> 10.9 us  [on_device(): lax.all_to_all(partial, split, split_axis=0, concat_axis=0, tiled=True)]
    all_to_all x0 -> x1, waiting for transfers between devices: none -> 5.07 us  [on_device(): lax.all_to_all(partial, split, split_axis=0, concat_axis=0, tiled=True)]
    unnamed x6 -> x4, local copies, waits for them, and re-layouts: 2.14 us -> 0.01 us
    pallas_call x1, Pallas kernels: 3.35 us -> 1.76 us  [unpack(): pl.pallas_call(body, grid=(outer // per_step,), in_specs=[pl.BlockSpec((g...]
    pallas_call x1, Pallas kernels: 3.31 us -> 1.8 us  [transform(): pl.pallas_call(body, in_specs=[pl.BlockSpec(memory_space=pltpu.SMEM), vme...]
  transfers between devices with their start and end apart: 2 -> 3, of which waited for: 1 -> 3; matrix products, arithmetic and copies ran while one was open for 2% -> 1% of each run, Pallas kernels for 0% -> 2%
where the time goes in v2:
time: 77 us; the launch traced here: 76.7 us
  waiting for transfers between devices  44.8 us (58%)
  starting transfers between devices  22.6 us (29%)
  Pallas kernels  6.16 us (8%)
  other arithmetic  1.54 us (2%)
  local copies, waits for them, and re-layouts  0.86 us (1%)
    all_to_all x1, waiting for transfers between devices, on_device(): lax.all_to_all(packed, 'ta', split_axis=0, concat_axis=0, tiled=True)  27.8 us
    all_to_all x1, waiting for transfers between devices, on_device(): lax.all_to_all(payload, 'ta', split_axis=0, concat_axis=0, tiled=True)  11.9 us
    all_to_all x1, starting transfers between devices, on_device(): lax.all_to_all(partial, split, split_axis=0, concat_axis=0, tiled=True)  10.9 us
    all_to_all x1, starting transfers between devices, on_device(): lax.all_to_all(packed, 'ta', split_axis=0, concat_axis=0, tiled=True)  7.58 us
    all_to_all x1, waiting for transfers between devices, on_device(): lax.all_to_all(partial, split, split_axis=0, concat_axis=0, tiled=True)  5.07 us
    all_to_all x1, starting transfers between devices, on_device(): lax.all_to_all(payload, 'ta', split_axis=0, concat_axis=0, tiled=True)  4.2 us
    pallas_call x1, Pallas kernels, pack(): pl.pallas_call(body, in_specs=[pl.BlockSpec(memory_space=pltpu.HBM)], out...  2.6 us
    pallas_call x1, Pallas kernels, transform(): pl.pallas_call(body, in_specs=[pl.BlockSpec(memory_space=pltpu.SMEM), vme...  1.8 us
  transfers between devices with their start and end apart: 3, of which 3 were waited for; matrix products, arithmetic and copies ran while one was open for 1% of the time, Pallas kernels for 2%

profile of v2, /device:TPU:1, one launch (start us, length us, event | category | flops | bytes accessed | tf_op | source)
XLA Modules:
  0.0 76.7 jit_solution(44856027048493163)
XLA Ops:
  0.6 2.6 %pack.1 = bf16[16,5,24,512]{3,2,1,0:T(8,128)(2,1)} custom-call(bf16[5,24,8192]{2,1,0:T(8,128)(2,1)} %bitcast.14), custom_call_target="tpu_custom_call" | custom-call | tf_op jit(solution)/shard_map/pack/pallas_call | solution.py:59
  3.2 0.0 copy-start.1
  3.2 0.0 copy-start
  3.3 7.6 %all-to-all-start = ((bf16[16,5,24,512]{3,2,1,0:T(8,128)(2,1)}), bf16[16,5,24,512]{3,2,1,0:T(8,128)(2,1)S(1)}, u32[]{:S(2)}, u32[]{:S(2)}) async-start(bf16[16,5,24,512]{3,2,1,0:T(8,128)(2,1)} %pack.1), calls=%async_computation | async-start | bytes 3932160 | tf_op jit(solution)/shard_map/all_to_all | solution.py:175
  10.9 0.0 copy-done.1
  10.9 0.1 reshape.129
  10.9 0.1 copy.11
  11.0 0.1 mul.102
  11.1 0.1 fusion.8
  11.3 0.1 iota_subtract_fusion
  11.3 0.5 multiply_convert_fusion.1
  11.8 27.8 %all-to-all-done.x_ref = bf16[16,5,24,512]{3,2,1,0:T(8,128)(2,1)S(1)} async-done(((bf16[16,5,24,512]{3,2,1,0:T(8,128)(2,1)}), bf16[16,5,24,512]{3,2,1,0:T(8,128)(2,1)S(1)}, u32[]{:S(2)}, u32[]{:S(2)}) %all-to-all-start) | async-done | bytes 1966112 | tf_op jit(solution)/shard_map/all_to_all | solution.py:175
  39.7 0.0 copy-done
  39.7 1.8 %transform.1 = bf16[2688,128]{1,0:T(8,128)(2,1)} custom-call(s32[1]{0:T(128)} %bitcast.g_ref, bf16[16,5,24,512]{3,2,1,0:T(8,128)(2,1)S(1)} %all-to-all-done.x_ref, bf16[128,384]{1,0:T(8,128)(2,1)S(1)} %bitcast.12, f32[64,128]{1,0:T(8,128)S(1)} %bitcast.13), custom_call_target="tpu_custom_call" | custom-call | tf_op jit(solution)/shard_map/transform/pallas_call | solution.py:119
  41.5 4.2 %all-to-all-start.1 = ((bf16[16,168,128]{2,1,0:T(8,128)(2,1)}), bf16[16,168,128]{2,1,0:T(8,128)(2,1)S(1)}, u32[]{:S(2)}, u32[]{:S(2)}) async-start(bf16[16,168,128]{2,1,0:T(8,128)(2,1)} %bitcast.5), calls=%async_computation.1 | async-start | bytes 1376256 | tf_op jit(solution)/shard_map/all_to_all | solution.py:178
  45.7 11.9 %all-to-all-done.1.y_ref = bf16[16,168,128]{2,1,0:T(8,128)(2,1)S(1)} async-done(((bf16[16,168,128]{2,1,0:T(8,128)(2,1)}), bf16[16,168,128]{2,1,0:T(8,128)(2,1)S(1)}, u32[]{:S(2)}, u32[]{:S(2)}) %all-to-all-start.1) | async-done | bytes 688160 | tf_op jit(solution)/shard_map/all_to_all | solution.py:178
  57.6 0.6 broadcast_in_dim.31
  58.2 10.9 %all-to-all-start.2 = ((f32[16,1,128]{2,1,0:T(1,128)}), f32[16,1,128]{2,1,0:T(1,128)S(1)}, u32[]{:S(2)}, u32[]{:S(2)}) async-start(f32[16,1,128]{2,1,0:T(1,128)} %broadcast_in_dim.31), calls=%async_computation.2 | async-start | bytes 16384 | tf_op jit(solution)/shard_map/all_to_all | solution.py:183
  69.1 1.8 %unpack.1 = f32[20,128,128]{2,1,0:T(8,128)} custom-call(bf16[16,168,128]{2,1,0:T(8,128)(2,1)S(1)} %all-to-all-done.1.y_ref), custom_call_target="tpu_custom_call" | custom-call | tf_op jit(solution)/shard_map/unpack/pallas_call | solution.py:142
  70.8 5.1 %all-to-all-done.2 = f32[16,1,128]{2,1,0:T(1,128)S(1)} async-done(((f32[16,1,128]{2,1,0:T(1,128)}), f32[16,1,128]{2,1,0:T(1,128)S(1)}, u32[]{:S(2)}, u32[]{:S(2)}) %all-to-all-start.2) | async-done | bytes 8224 | tf_op jit(solution)/shard_map/all_to_all | solution.py:183
  75.9 0.8 fusion.4
  (6 shorter events, 0.1 us)
Async XLA Ops:
  3.2 7.6 %copy-start.1 = (s32[32]{0:T(128)S(1)}, s32[32]{0:T(128)}, u32[]{:S(2)}) copy-start(s32[32]{0:T(128)} %param.5) | copy-start | bytes 388
  3.2 36.4 %copy-start = (f32[8192]{0:T(1024)S(1)}, f32[8192]{0:T(1024)}, u32[]{:S(2)}) copy-start(f32[8192]{0:T(1024)} %param.4) | copy-start | bytes 98308
  3.3 36.4 %all-to-all-start = ((bf16[16,5,24,512]{3,2,1,0:T(8,128)(2,1)}), bf16[16,5,24,512]{3,2,1,0:T(8,128)(2,1)S(1)}, u32[]{:S(2)}, u32[]{:S(2)}) async-start(bf16[16,5,24,512]{3,2,1,0:T(8,128)(2,1)} %pack.1), calls=%async_computation | async-start | bytes 3932160 | tf_op jit(solution)/shard_map/all_to_all | solution.py:175
  41.5 16.1 %all-to-all-start.1 = ((bf16[16,168,128]{2,1,0:T(8,128)(2,1)}), bf16[16,168,128]{2,1,0:T(8,128)(2,1)S(1)}, u32[]{:S(2)}, u32[]{:S(2)}) async-start(bf16[16,168,128]{2,1,0:T(8,128)(2,1)} %bitcast.5), calls=%async_computation.1 | async-start | bytes 1376256 | tf_op jit(solution)/shard_map/all_to_all | solution.py:178
  58.2 17.7 %all-to-all-start.2 = ((f32[16,1,128]{2,1,0:T(1,128)}), f32[16,1,128]{2,1,0:T(1,128)S(1)}, u32[]{:S(2)}, u32[]{:S(2)}) async-start(f32[16,1,128]{2,1,0:T(1,128)} %broadcast_in_dim.31), calls=%async_computation.2 | async-start | bytes 16384 | tf_op jit(solution)/shard_map/all_to_all | solution.py:183

commit v3 on v2

v3 whole, which is shorter than its diff:
```python
import math

import jax
import jax.numpy as jnp
import numpy as np
from jax import lax
from jax.experimental import pallas as pl
from jax.experimental.pallas import tpu as pltpu
from jax.sharding import PartitionSpec as P


VARS = 5
BLK = 256
HOP = 128
SEGMENT_NUMBER = 2
RECORD_LENGTH = 384
RETAINED_MODES = 32
LANES = 128
VMEM_LIMIT = 16 << 20
EXTRA = 8


def multipliers_of(index_ref, own):
    modes = index_ref.shape[0]
    places = modes // own
    row = lax.broadcasted_iota(jnp.int32, (modes, BLK), 0)
    lag = lax.broadcasted_iota(jnp.int32, (modes, BLK), 1)
    index = jnp.zeros((modes, BLK), jnp.int32)
    for f in range(modes):
        index = jnp.where(row == f % own * places + f // own, index_ref[f], index)
    window = 0.5 - 0.5 * jnp.cos(2.0 * math.pi * lag.astype(jnp.float32) / BLK)
    window = window / jnp.sqrt(jnp.float32(3.0 * BLK / 8.0))
    angles = 2.0 * math.pi * ((index * lag) & (BLK - 1)).astype(jnp.float32) / BLK
    return jnp.cos(angles) * window, -jnp.sin(angles) * window


def pack(shard, indices, weights, me, groups):
    variables, times, points = shard.shape
    piece = points // groups
    modes = indices.shape[0]

    tiles = piece // LANES

    def body(me_ref, index_hbm, w_hbm, x_hbm, o_ref, m_ref, r_ref, index_ref, w_ref, sem, index_sem, w_sem):
        get_index = pltpu.make_async_copy(index_hbm, index_ref, index_sem)
        get_weights = pltpu.make_async_copy(w_hbm, w_ref, w_sem)
        get_index.start()
        copies = [
            pltpu.make_async_copy(x_hbm.at[:, :, pl.ds(d * piece, piece)], o_ref.at[d], sem.at[d])
            for d in range(groups)
        ]
        for copy in copies:
            copy.start()
        get_weights.start()
        m_ref[...] = jnp.zeros_like(m_ref)
        get_index.wait()
        for c, part in enumerate(multipliers_of(index_ref, modes // groups)):
            for b in range(SEGMENT_NUMBER):
                at = (c * SEGMENT_NUMBER + b) * modes
                m_ref[at : at + modes, b * HOP : b * HOP + BLK] = part.astype(m_ref.dtype)
        get_weights.wait()
        r_ref[...] = jnp.sqrt(w_ref[pl.ds(me_ref[0] * tiles, tiles), :])
        for copy in copies:
            copy.wait()

    vmem = pl.BlockSpec(memory_space=pltpu.VMEM)
    smem = pl.BlockSpec(memory_space=pltpu.SMEM)
    hbm = pl.BlockSpec(memory_space=pltpu.HBM)
    arrays = [pltpu.with_memory_space_constraint(array, pltpu.HBM) for array in (indices, weights, shard)]
    return pl.pallas_call(
        body,
        in_specs=[smem, hbm, hbm, hbm],
        out_specs=(vmem, vmem, vmem),
        out_shape=(
            jax.ShapeDtypeStruct((groups, variables, times, piece), shard.dtype),
            jax.ShapeDtypeStruct((2 * SEGMENT_NUMBER * modes, RECORD_LENGTH), jnp.bfloat16),
            jax.ShapeDtypeStruct((tiles, LANES), jnp.float32),
        ),
        scratch_shapes=[
            pltpu.SMEM(indices.shape, indices.dtype),
            pltpu.VMEM(weights.shape, weights.dtype),
            pltpu.SemaphoreType.DMA((groups,)),
            pltpu.SemaphoreType.DMA,
            pltpu.SemaphoreType.DMA,
        ],
        compiler_params=pltpu.CompilerParams(vmem_limit_bytes=VMEM_LIMIT),
        name="pack",
    )(me, *arrays)


def transform(gathered, multipliers, roots):
    groups, variables, times, piece = gathered.shape
    tiles = piece // LANES
    modes = RETAINED_MODES
    own = modes // groups
    per_mode = SEGMENT_NUMBER * variables * tiles * 2
    height = own * per_mode + EXTRA

    def body(x_ref, m_ref, r_ref, z_ref, f_ref, acc_ref):
        m = m_ref[...]
        acc_ref[...] = jnp.zeros_like(acc_ref)
        for v in range(variables):
            x = x_ref[:, v].reshape(groups * times, piece)
            s = jnp.dot(m, x, preferred_element_type=jnp.float32)
            for j in range(tiles):
                q = s[:, j * LANES : (j + 1) * LANES] * r_ref[j : j + 1, :]
                parts = {}
                for c in range(2):
                    for b in range(SEGMENT_NUMBER):
                        at = (c * SEGMENT_NUMBER + b) * modes
                        part = q[at : at + modes]
                        parts[c, b] = part
                        for k in range(own):
                            first = k * per_mode + (b * variables + v) * tiles * 2 + j * 2 + c
                            f_ref[pl.ds(first, groups, stride=height), :] = part[k * groups : (k + 1) * groups]
                r0, r1, i0, i1 = parts[0, 0], parts[0, 1], parts[1, 0], parts[1, 1]
                acc_ref[0:modes] += r0 * r0 + i0 * i0
                acc_ref[modes : 2 * modes] += r1 * r1 + i1 * i1
                acc_ref[2 * modes : 3 * modes] += r0 * r1 + i0 * i1
                acc_ref[3 * modes : 4 * modes] += r0 * i1 - i0 * r1
        total = lax.dot_general(
            jnp.ones((EXTRA, LANES), jnp.float32),
            acc_ref[...],
            (((1,), (1,)), ((), ())),
            precision=lax.Precision.HIGHEST,
            preferred_element_type=jnp.float32,
        )
        rounded = total.astype(jnp.bfloat16).astype(jnp.float32)
        row = lax.broadcasted_iota(jnp.int32, total.shape, 0)
        tail = jnp.where(row == 0, rounded, jnp.where(row == 1, total - rounded, 0.0))
        for d in range(groups):
            f_ref[d * height + own * per_mode : (d + 1) * height, :] = tail
        z_ref[...] = f_ref[...].reshape(z_ref.shape).astype(z_ref.dtype)

    vmem = pl.BlockSpec(memory_space=pltpu.VMEM)
    return pl.pallas_call(
        body,
        in_specs=[vmem, vmem, vmem],
        out_specs=vmem,
        out_shape=jax.ShapeDtypeStruct((groups, height, LANES), jnp.bfloat16),
        scratch_shapes=[
            pltpu.VMEM((groups * height, LANES), jnp.float32),
            pltpu.VMEM((4 * modes, LANES), jnp.float32),
        ],
        compiler_params=pltpu.CompilerParams(vmem_limit_bytes=VMEM_LIMIT),
        name="transform",
    )(gathered, multipliers, roots)


def unpack(received, rows, inner):
    groups, _, lanes = received.shape
    outer = rows // inner
    per_step = 5

    def body(y_ref, o_ref):
        for s in range(groups):
            o_ref[:, s * inner : (s + 1) * inner, :] = y_ref[s].astype(jnp.float32).reshape(per_step, inner, lanes)

    return pl.pallas_call(
        body,
        grid=(outer // per_step,),
        in_specs=[pl.BlockSpec((groups, per_step * inner, lanes), lambda k: (0, k, 0))],
        out_specs=pl.BlockSpec((per_step, groups * inner, lanes), lambda k: (k, 0, 0)),
        out_shape=jax.ShapeDtypeStruct((outer, groups * inner, lanes), jnp.float32),
        compiler_params=pltpu.CompilerParams(vmem_limit_bytes=VMEM_LIMIT),
        name="unpack",
    )(received)


def sum_over(value, axis):
    size = lax.axis_size(axis)
    halvings = (1, 2, 6) if size == 8 else tuple(1 << k for k in range(size.bit_length() - 1))
    for apart in halvings:
        value = value + lax.ppermute(value, axis, [(d, d ^ apart) for d in range(size)])
    return value


def gram_of(sums, me, own, terms):
    shape = (own, SEGMENT_NUMBER, SEGMENT_NUMBER, 2, 1)
    f, b, b2, part, _ = np.indices(shape)
    first = (np.where(b == b2, b, 2 + part) * own + f) * (RETAINED_MODES // own)
    factor = np.where(part == 0, 1.0, b2 - b) / terms
    lane = lax.broadcasted_iota(jnp.int32, shape[:4] + (LANES,), 4)
    chosen = jnp.where(lane == jnp.asarray(first, jnp.int32) + me, sums, 0.0)
    return jnp.sum(chosen * jnp.asarray(factor, jnp.float32), axis=-1)


def on_device(snapshots, quad_weights, spectral_indices):
    point_count = snapshots.shape[2]
    groups = lax.axis_size("ta")
    me = lax.axis_index("ta").astype(jnp.int32)
    own = RETAINED_MODES // groups
    tiles = point_count // groups // LANES
    rows = own * SEGMENT_NUMBER * VARS * tiles * 2

    weights = quad_weights.reshape(point_count // LANES, LANES)
    packed, multipliers, roots = pack(jnp.transpose(snapshots, (1, 0, 2)), spectral_indices, weights, me[None], groups)
    gathered = lax.all_to_all(packed, "ta", split_axis=0, concat_axis=0, tiled=True)
    payload = transform(gathered, multipliers, roots)
    received = lax.all_to_all(payload, "ta", split_axis=0, concat_axis=0, tiled=True)

    sums = jnp.sum(received[:, rows : rows + 2].astype(jnp.float32), axis=0)
    sums = jnp.sum(sums, axis=0, keepdims=True)
    for axis in ("px", "py"):
        sums = sum_over(sums, axis)
    terms = point_count * lax.axis_size("px") * lax.axis_size("py") * VARS
    gram = gram_of(sums, me, own, terms)

    spectra = unpack(received, rows, tiles * 2)
    spectra = spectra.reshape(own, SEGMENT_NUMBER, VARS, point_count // LANES, 2, LANES)
    spectra = jnp.transpose(spectra, (0, 1, 4, 2, 3, 5)).reshape(own, SEGMENT_NUMBER, 2, VARS, point_count)
    return (spectra, gram)


def solution(mesh):
    return jax.shard_map(
        on_device,
        mesh=mesh,
        in_specs=(P("ta", None, ("px", "py")), P(("px", "py")), P()),
        out_specs=(P("ta", None, None, None, ("px", "py")), P("ta", None, None, None)),
        check_vma=False,
    )
```

time: 77 us -> 70.2 us (0.912)
  blocking collectives: 0 us -> 48.2 us
  waiting for transfers between devices: 44.8 us -> 2.73 us
  starting transfers between devices: 22.6 us -> 12.6 us
  Pallas kernels: 6.16 us -> 4.45 us
  local copies, waits for them, and re-layouts: 0.86 us -> 0.03 us
    all_to_all x0 -> x2, blocking collectives: none -> 48.2 us  [the longest x1 33.5 us: on_device(): lax.all_to_all(packed, 'ta', split_axis=0, concat_axis=0, tiled=True)]
    all_to_all x3 -> x0, waiting for transfers between devices: 44.8 us -> none  [the longest x1 27.8 us: on_device(): lax.all_to_all(packed, 'ta', split_axis=0, concat_axis=0, tiled=True)]
    all_to_all x3 -> x0, starting transfers between devices: 22.6 us -> none  [the longest x1 10.9 us: on_device(): lax.all_to_all(partial, split, split_axis=0, concat_axis=0, tiled=True)]
    ppermute x0 -> x4, starting transfers between devices: none -> 12.6 us  [sum_over(): lax.ppermute(value, axis, [(d, d ^ apart) for d in range(size)])]
    ppermute x0 -> x4, waiting for transfers between devices: none -> 2.73 us  [sum_over(): lax.ppermute(value, axis, [(d, d ^ apart) for d in range(size)])]
    pallas_call x2, Pallas kernels: 4.4 us -> 2.71 us  [the longest x1 1.75 us: pack(): pl.pallas_call(body, in_specs=[smem, hbm, hbm, hbm], out_specs=(vmem, vme...]
  transfers between devices with their start and end apart: 3 -> 4, of which waited for: 3 -> 3; matrix products, arithmetic and copies ran while one was open for 1% -> 0% of each run, Pallas kernels for 2% -> 3%
where the time goes in v3:
time: 70.2 us; the launch traced here: 69.5 us
  blocking collectives  48.2 us (69%)
  starting transfers between devices  12.6 us (18%)
  Pallas kernels  4.45 us (6%)
  waiting for transfers between devices  2.73 us (4%)
  other arithmetic  0.82 us (1%)
    all_to_all x1, blocking collectives, on_device(): lax.all_to_all(packed, 'ta', split_axis=0, concat_axis=0, tiled=True)  33.5 us
    all_to_all x1, blocking collectives, on_device(): lax.all_to_all(payload, 'ta', split_axis=0, concat_axis=0, tiled=True)  14.7 us
    ppermute x4, starting transfers between devices, sum_over(): lax.ppermute(value, axis, [(d, d ^ apart) for d in range(size)])  12.6 us
    ppermute x4, waiting for transfers between devices, sum_over(): lax.ppermute(value, axis, [(d, d ^ apart) for d in range(size)])  2.73 us
    pallas_call x1, Pallas kernels, pack(): pl.pallas_call(body, in_specs=[smem, hbm, hbm, hbm], out_specs=(vmem, vme...  1.75 us
    pallas_call x1, Pallas kernels, unpack(): pl.pallas_call(body, grid=(outer // per_step,), in_specs=[pl.BlockSpec((g...  1.74 us
  transfers between devices with their start and end apart: 4, of which 3 were waited for; matrix products, arithmetic and copies ran while one was open for 0% of the time, Pallas kernels for 3%

profile of v3, /device:TPU:1, one launch (start us, length us, event | category | flops | bytes accessed | tf_op | source)
XLA Modules:
  0.0 69.5 jit_solution(9519346966176880539)
XLA Ops:
  0.6 1.7 %pack.1 = (bf16[16,5,24,512]{3,2,1,0:T(8,128)(2,1)S(1)}, bf16[128,384]{1,0:T(8,128)(2,1)S(1)}, f32[4,128]{1,0:T(4,128)S(1)}) custom-call(s32[1]{0:T(128)} %bitcast.me_ref, s32[32]{0:T(128)} %index_hbm.1, f32[64,128]{1,0:T(8,128)} %bitcast.16, bf16[5,24,8192]{2,1,0:T(8,128)(2,1)} %bitcast.14), custom_call_target="tpu_custom_call" | custom-call | tf_op jit(solution)/shard_map/pack/pallas_call | solution.py:70
  2.4 33.5 %all_to_all.10.x_ref = bf16[16,5,24,512]{3,2,1,0:T(8,128)(2,1)S(1)} all-to-all(bf16[16,5,24,512]{3,2,1,0:T(8,128)(2,1)S(1)} %get-tuple-element.5), channel_id=1, replica_groups=mesh['px'=2,'py'=8,'ta'=16] {'ta'}, dimensions={0} | all-to-all | bytes 3932160 | tf_op jit(solution)/shard_map/all_to_all | solution.py:198
  35.9 0.0 copy-start.1
  35.9 1.0 %transform.1 = bf16[16,168,128]{2,1,0:T(8,128)(2,1)S(1)} custom-call(bf16[16,5,24,512]{3,2,1,0:T(8,128)(2,1)S(1)} %all_to_all.10.x_ref, bf16[128,384]{1,0:T(8,128)(2,1)S(1)} %get-tuple-element.6.m_ref, f32[4,128]{1,0:T(4,128)S(1)} %get-tuple-element.7.r_ref), custom_call_target="tpu_custom_call" | custom-call | tf_op jit(solution)/shard_map/transform/pallas_call | solution.py:136
  36.9 0.0 copy-start
  36.9 14.7 %all_to_all.11.y_ref = bf16[16,168,128]{2,1,0:T(8,128)(2,1)S(1)} all-to-all(bf16[16,168,128]{2,1,0:T(8,128)(2,1)S(1)} %transform.1), channel_id=1, replica_groups=mesh['px'=2,'py'=8,'ta'=16] {'ta'}, dimensions={0} | all-to-all | bytes 1376256 | tf_op jit(solution)/shard_map/all_to_all | solution.py:200
  51.6 2.7 %collective-permute-start = (f32[1,128]{1,0:T(1,128)S(1)}, f32[1,128]{1,0:T(1,128)S(1)}, u32[]{:S(2)}, u32[]{:S(2)}) collective-permute-start(f32[1,128]{1,0:T(1,128)S(1)} %bitcast.17), channel_id=1, source_target_pairs={{0,128},{128,0},{1,129},{129,1},{2,130},{130,2},{3,131},{131,3},{4... | collective-permute-start | bytes 1544 | tf_op jit(solution)/shard_map/ppermute | solution.py:174
  54.4 0.8 %collective-permute-done = f32[1,128]{1,0:T(1,128)S(1)} collective-permute-done((f32[1,128]{1,0:T(1,128)S(1)}, f32[1,128]{1,0:T(1,128)S(1)}, u32[]{:S(2)}, u32[]{:S(2)}) %collective-permute-start) | collective-permute-done | bytes 544 | tf_op jit(solution)/shard_map/ppermute | solution.py:174
  55.2 1.6 %collective-permute-start.1 = (f32[1,128]{1,0:T(1,128)S(1)}, f32[1,128]{1,0:T(1,128)S(1)}, u32[]{:S(2)}, u32[]{:S(2)}) collective-permute-start(f32[1,128]{1,0:T(1,128)S(1)} %bitcast_add_fusion), channel_id=1, source_target_pairs={{0,16},{16,0},{32,48},{48,32},{64,80},{80,64},{96,112},{112,96},{1... | collective-permute-start | bytes 1544 | tf_op jit(solution)/shard_map/ppermute | solution.py:174
  56.8 1.0 %collective-permute-done.1 = f32[1,128]{1,0:T(1,128)S(1)} collective-permute-done((f32[1,128]{1,0:T(1,128)S(1)}, f32[1,128]{1,0:T(1,128)S(1)}, u32[]{:S(2)}, u32[]{:S(2)}) %collective-permute-start.1) | collective-permute-done | bytes 544 | tf_op jit(solution)/shard_map/ppermute | solution.py:174
  57.8 3.0 %collective-permute-start.2 = (f32[1,128]{1,0:T(1,128)S(1)}, f32[1,128]{1,0:T(1,128)S(1)}, u32[]{:S(2)}, u32[]{:S(2)}) collective-permute-start(f32[1,128]{1,0:T(1,128)S(1)} %add.23), channel_id=1, source_target_pairs={{0,32},{16,48},{32,0},{48,16},{64,96},{80,112},{96,64},{112,80},{1... | collective-permute-start | bytes 1544 | tf_op jit(solution)/shard_map/ppermute | solution.py:174
  60.8 1.0 %collective-permute-done.2 = f32[1,128]{1,0:T(1,128)S(1)} collective-permute-done((f32[1,128]{1,0:T(1,128)S(1)}, f32[1,128]{1,0:T(1,128)S(1)}, u32[]{:S(2)}, u32[]{:S(2)}) %collective-permute-start.2) | collective-permute-done | bytes 544 | tf_op jit(solution)/shard_map/ppermute | solution.py:174
  61.7 5.2 %collective-permute-start.3 = (f32[1,128]{1,0:T(1,128)S(1)}, f32[1,128]{1,0:T(1,128)S(1)}, u32[]{:S(2)}, u32[]{:S(2)}) collective-permute-start(f32[1,128]{1,0:T(1,128)S(1)} %add.24), channel_id=1, source_target_pairs={{0,96},{16,112},{32,64},{48,80},{64,32},{80,48},{96,0},{112,16},{1... | collective-permute-start | bytes 1544 | tf_op jit(solution)/shard_map/ppermute | solution.py:174
  66.9 0.0 copy-done.1
  67.0 1.7 %unpack.1 = f32[20,128,128]{2,1,0:T(8,128)} custom-call(bf16[16,168,128]{2,1,0:T(8,128)(2,1)S(1)} %all_to_all.11.y_ref), custom_call_target="tpu_custom_call" | custom-call | tf_op jit(solution)/shard_map/unpack/pallas_call | solution.py:159
  68.7 0.0 collective-permute-done.3
  68.7 0.0 copy-done
  68.7 0.8 %fusion.1 = f32[2,2,2,2]{3,2,1,0:T(2,128)} fusion(f32[2,2,2,2]{3,2,1,0:T(2,128)S(1)} %copy-done, f32[128]{0:T(128)S(1)} %add_bitcast_fusion.1, s32[2,2,2,2]{3,2,1,0:T(2,128)S(1)} %add_bitcast_fusion), kind=kLoop, calls=%fused_computation.3 | loop fusion | flops 8176 | bytes 704 | tf_op jit(solution)/shard_map/reduce_sum | solution.py:185
  (6 shorter events, 0.1 us)
Async XLA Ops:
  35.9 31.0 %copy-start.1 = (s32[2,2,2,2,1]{3,2,1,0,4:T(2,128)S(1)}, s32[2,2,2,2,1]{3,2,1,0,4:T(2,128)}, u32[]{:S(2)}) copy-start(s32[2,2,2,2,1]{3,2,1,0,4:T(2,128)} %constant.10.clone) | copy-start | bytes 196
  36.9 31.8 %copy-start = (f32[2,2,2,2]{3,2,1,0:T(2,128)S(1)}, f32[2,2,2,2]{3,2,1,0:T(2,128)}, u32[]{:S(2)}) copy-start(f32[2,2,2,2]{3,2,1,0:T(2,128)} %constant.13) | copy-start | bytes 196
  51.6 3.5 %collective-permute-start = (f32[1,128]{1,0:T(1,128)S(1)}, f32[1,128]{1,0:T(1,128)S(1)}, u32[]{:S(2)}, u32[]{:S(2)}) collective-permute-start(f32[1,128]{1,0:T(1,128)S(1)} %bitcast.17), channel_id=1, source_target_pairs={{0,128},{128,0},{1,129},{129,1},{2,130},{130,2},{3,131},{131,3},{4... | collective-permute-start | bytes 1544 | tf_op jit(solution)/shard_map/ppermute | solution.py:174
  55.2 2.6 %collective-permute-start.1 = (f32[1,128]{1,0:T(1,128)S(1)}, f32[1,128]{1,0:T(1,128)S(1)}, u32[]{:S(2)}, u32[]{:S(2)}) collective-permute-start(f32[1,128]{1,0:T(1,128)S(1)} %bitcast_add_fusion), channel_id=1, source_target_pairs={{0,16},{16,0},{32,48},{48,32},{64,80},{80,64},{96,112},{112,96},{1... | collective-permute-start | bytes 1544 | tf_op jit(solution)/shard_map/ppermute | solution.py:174
  57.8 3.9 %collective-permute-start.2 = (f32[1,128]{1,0:T(1,128)S(1)}, f32[1,128]{1,0:T(1,128)S(1)}, u32[]{:S(2)}, u32[]{:S(2)}) collective-permute-start(f32[1,128]{1,0:T(1,128)S(1)} %add.23), channel_id=1, source_target_pairs={{0,32},{16,48},{32,0},{48,16},{64,96},{80,112},{96,64},{112,80},{1... | collective-permute-start | bytes 1544 | tf_op jit(solution)/shard_map/ppermute | solution.py:174
  61.7 7.0 %collective-permute-start.3 = (f32[1,128]{1,0:T(1,128)S(1)}, f32[1,128]{1,0:T(1,128)S(1)}, u32[]{:S(2)}, u32[]{:S(2)}) collective-permute-start(f32[1,128]{1,0:T(1,128)S(1)} %add.24), channel_id=1, source_target_pairs={{0,96},{16,112},{32,64},{48,80},{64,32},{80,48},{96,0},{112,16},{1... | collective-permute-start | bytes 1544 | tf_op jit(solution)/shard_map/ppermute | solution.py:174

commit v4 on v3

--- a/solution.py
+++ b/solution.py
@@ -18,6 +18,24 @@
 LANES = 128
 VMEM_LIMIT = 16 << 20
 EXTRA = 8
+SPREAD = (9, 7, 13, 11, 10, 5, 2, 0, 15, 14, 4, 3, 6, 12, 1, 8)
+COLLECT = (9, 7, 13, 11, 10, 5, 2, 0, 15, 14, 4, 3, 6, 12, 1, 8)
+POINTS = (12, 0, 1, 2, 3, 4, 5, 6, 7, 8, 9, 10, 11, 13, 14, 15)
+
+
+def slots(order):
+    return [order.index(d) for d in range(len(order))]
+
+
+def slot_of(device, order):
+    words = [sum(slot << 4 * k for k, slot in enumerate(slots(order)[at : at + 7])) for at in (0, 7, 14)]
+    word = jnp.where(device < 7, words[0], jnp.where(device < 14, words[1], words[2]))
+    return lax.shift_right_logical(word, 4 * lax.rem(device, 7)) & 15
+
+
+def exchange(pieces, axes, order):
+    groups = [list(order)] if len(order) == pieces.shape[0] else None
+    return lax.all_to_all(pieces, axes, split_axis=0, concat_axis=0, tiled=True, axis_index_groups=groups)
 
 
 def multipliers_of(index_ref, own):
@@ -27,26 +45,26 @@
     lag = lax.broadcasted_iota(jnp.int32, (modes, BLK), 1)
     index = jnp.zeros((modes, BLK), jnp.int32)
     for f in range(modes):
-        index = jnp.where(row == f % own * places + f // own, index_ref[f], index)
+        index = jnp.where(row == f % own * places + slots(COLLECT)[f // own], index_ref[f], index)
     window = 0.5 - 0.5 * jnp.cos(2.0 * math.pi * lag.astype(jnp.float32) / BLK)
     window = window / jnp.sqrt(jnp.float32(3.0 * BLK / 8.0))
     angles = 2.0 * math.pi * ((index * lag) & (BLK - 1)).astype(jnp.float32) / BLK
     return jnp.cos(angles) * window, -jnp.sin(angles) * window
 
 
-def pack(shard, indices, weights, me, groups):
+def pack(shard, indices, weights, places, groups):
     variables, times, points = shard.shape
     piece = points // groups
     modes = indices.shape[0]
 
     tiles = piece // LANES
 
-    def body(me_ref, index_hbm, w_hbm, x_hbm, o_ref, m_ref, r_ref, index_ref, w_ref, sem, index_sem, w_sem):
+    def body(places_ref, index_hbm, w_hbm, x_hbm, o_ref, m_ref, r_ref, index_ref, w_ref, sem, index_sem, w_sem):
         get_index = pltpu.make_async_copy(index_hbm, index_ref, index_sem)
         get_weights = pltpu.make_async_copy(w_hbm, w_ref, w_sem)
         get_index.start()
         copies = [
-            pltpu.make_async_copy(x_hbm.at[:, :, pl.ds(d * piece, piece)], o_ref.at[d], sem.at[d])
+            pltpu.make_async_copy(x_hbm.at[:, :, pl.ds(d * piece, piece)], o_ref.at[slots(SPREAD)[d]], sem.at[d])
             for d in range(groups)
         ]
         for copy in copies:
@@ -59,7 +77,8 @@
                 at = (c * SEGMENT_NUMBER + b) * modes
                 m_ref[at : at + modes, b * HOP : b * HOP + BLK] = part.astype(m_ref.dtype)
         get_weights.wait()
-        r_ref[...] = jnp.sqrt(w_ref[pl.ds(me_ref[0] * tiles, tiles), :])
+        me = lax.div(places_ref[0], groups)
+        r_ref[...] = jnp.sqrt(w_ref[pl.ds(me * tiles, tiles), :])
         for copy in copies:
             copy.wait()
 
@@ -85,11 +104,11 @@
         ],
         compiler_params=pltpu.CompilerParams(vmem_limit_bytes=VMEM_LIMIT),
         name="pack",
-    )(me, *arrays)
+    )(places, *arrays)
 
 
 def transform(gathered, multipliers, roots):
-    groups, variables, times, piece = gathered.shape
+    groups, variables, _, piece = gathered.shape
     tiles = piece // LANES
     modes = RETAINED_MODES
     own = modes // groups
@@ -100,7 +119,7 @@
         m = m_ref[...]
         acc_ref[...] = jnp.zeros_like(acc_ref)
         for v in range(variables):
-            x = x_ref[:, v].reshape(groups * times, piece)
+            x = jnp.concatenate([x_ref[slot, v] for slot in slots(SPREAD)], axis=0)
             s = jnp.dot(m, x, preferred_element_type=jnp.float32)
             for j in range(tiles):
                 q = s[:, j * LANES : (j + 1) * LANES] * r_ref[j : j + 1, :]
@@ -154,7 +173,7 @@
 
     def body(y_ref, o_ref):
         for s in range(groups):
-            o_ref[:, s * inner : (s + 1) * inner, :] = y_ref[s].astype(jnp.float32).reshape(per_step, inner, lanes)
+            o_ref[:, s * inner : (s + 1) * inner, :] = y_ref[slots(COLLECT)[s]].astype(jnp.float32).reshape(per_step, inner, lanes)
 
     return pl.pallas_call(
         body,
@@ -167,21 +186,13 @@
     )(received)
 
 
-def sum_over(value, axis):
-    size = lax.axis_size(axis)
-    halvings = (1, 2, 6) if size == 8 else tuple(1 << k for k in range(size.bit_length() - 1))
-    for apart in halvings:
-        value = value + lax.ppermute(value, axis, [(d, d ^ apart) for d in range(size)])
-    return value
-
-
-def gram_of(sums, me, own, terms):
+def gram_of(sums, slot, own, terms):
     shape = (own, SEGMENT_NUMBER, SEGMENT_NUMBER, 2, 1)
     f, b, b2, part, _ = np.indices(shape)
     first = (np.where(b == b2, b, 2 + part) * own + f) * (RETAINED_MODES // own)
     factor = np.where(part == 0, 1.0, b2 - b) / terms
     lane = lax.broadcasted_iota(jnp.int32, shape[:4] + (LANES,), 4)
-    chosen = jnp.where(lane == jnp.asarray(first, jnp.int32) + me, sums, 0.0)
+    chosen = jnp.where(lane == jnp.asarray(first, jnp.int32) + slot, sums, 0.0)
     return jnp.sum(chosen * jnp.asarray(factor, jnp.float32), axis=-1)
 
 
@@ -194,17 +205,20 @@
     rows = own * SEGMENT_NUMBER * VARS * tiles * 2
 
     weights = quad_weights.reshape(point_count // LANES, LANES)
-    packed, multipliers, roots = pack(jnp.transpose(snapshots, (1, 0, 2)), spectral_indices, weights, me[None], groups)
-    gathered = lax.all_to_all(packed, "ta", split_axis=0, concat_axis=0, tiled=True)
+    slot = slot_of(me, COLLECT)
+    places = (me * groups + slot)[None]
+    packed, multipliers, roots = pack(jnp.transpose(snapshots, (1, 0, 2)), spectral_indices, weights, places, groups)
+    gathered = exchange(packed, "ta", SPREAD)
     payload = transform(gathered, multipliers, roots)
-    received = lax.all_to_all(payload, "ta", split_axis=0, concat_axis=0, tiled=True)
-
-    sums = jnp.sum(received[:, rows : rows + 2].astype(jnp.float32), axis=0)
-    sums = jnp.sum(sums, axis=0, keepdims=True)
-    for axis in ("px", "py"):
-        sums = sum_over(sums, axis)
-    terms = point_count * lax.axis_size("px") * lax.axis_size("py") * VARS
-    gram = gram_of(sums, me, own, terms)
+    received = exchange(payload, "ta", COLLECT)
+
+    split = ("px", "py")
+    copies = lax.axis_size(split)
+    sums = jnp.sum(received[:, rows : rows + 2].astype(jnp.float32), axis=(0, 1))
+    sums = jnp.broadcast_to(sums, (copies, 1, LANES))
+    sums = jnp.sum(exchange(sums, split, POINTS), axis=0)
+    terms = point_count * copies * VARS
+    gram = gram_of(sums, slot, own, terms)
 
     spectra = unpack(received, rows, tiles * 2)
     spectra = spectra.reshape(own, SEGMENT_NUMBER, VARS, point_count // LANES, 2, LANES)

time: 70.2 us -> 65.4 us (0.932)
  waiting for transfers between devices: 2.73 us -> 0.29 us
  blocking collectives: 48.2 us -> 46.8 us
  starting transfers between devices: 12.6 us -> 11.5 us
    ppermute x4 -> x0, starting transfers between devices: 12.6 us -> none  [sum_over(): lax.ppermute(value, axis, [(d, d ^ apart) for d in range(size)])]
    all_to_all x0 -> x1, starting transfers between devices: none -> 11.5 us  [exchange(): lax.all_to_all(pieces, axes, split_axis=0, concat_axis=0, tiled=True, axi...]
    ppermute x4 -> x0, waiting for transfers between devices: 2.73 us -> none  [sum_over(): lax.ppermute(value, axis, [(d, d ^ apart) for d in range(size)])]
    all_to_all x2, blocking collectives: 48.2 us -> 46.8 us  [exchange(): lax.all_to_all(pieces, axes, split_axis=0, concat_axis=0, tiled=True, axi...]
  transfers between devices with their start and end apart: 4 -> 1, of which waited for: 3 -> 1; matrix products, arithmetic and copies ran while one was open for 0% -> 0% of each run, Pallas kernels for 3% -> 3%
where the time goes in v4:
time: 65.4 us; the launch traced here: 65.2 us
  blocking collectives  46.8 us (72%)
  starting transfers between devices  11.5 us (18%)
  Pallas kernels  4.47 us (7%)
  other arithmetic  0.83 us (1%)
  between operations  0.68 us (1%)
    all_to_all x2, blocking collectives, exchange(): lax.all_to_all(pieces, axes, split_axis=0, concat_axis=0, tiled=True, axi...  46.8 us
    all_to_all x1, starting transfers between devices, exchange(): lax.all_to_all(pieces, axes, split_axis=0, concat_axis=0, tiled=True, axi...  11.5 us
    pallas_call x1, Pallas kernels, unpack(): pl.pallas_call(body, grid=(outer // per_step,), in_specs=[pl.BlockSpec((g...  1.76 us
    pallas_call x1, Pallas kernels, pack(): pl.pallas_call(body, in_specs=[smem, hbm, hbm, hbm], out_specs=(vmem, vme...  1.76 us
  transfers between devices with their start and end apart: 1, of which 1 were waited for; matrix products, arithmetic and copies ran while one was open for 0% of the time, Pallas kernels for 3%

profile of v4, /device:TPU:1, one launch (start us, length us, event | category | flops | bytes accessed | tf_op | source)
XLA Modules:
  0.0 65.2 jit_solution(6076964455275623488)
XLA Ops:
  0.7 1.8 %pack.1 = (bf16[16,5,24,512]{3,2,1,0:T(8,128)(2,1)S(1)}, bf16[128,384]{1,0:T(8,128)(2,1)S(1)}, f32[4,128]{1,0:T(4,128)S(1)}) custom-call(s32[1]{0:T(128)} %bitcast.places_ref, s32[32]{0:T(128)} %index_hbm.1, f32[64,128]{1,0:T(8,128)} %bitcast.13, bf16[5,24,8192]{2,1,0:T(8,128)(2,1)} %bitcast.11), custom_call_target="tpu_custom_call" | custom-call | tf_op jit(solution)/shard_map/pack/pallas_call | solution.py:89
  2.4 30.6 %all_to_all.15.x_ref = bf16[16,5,24,512]{3,2,1,0:T(8,128)(2,1)S(1)} all-to-all(bf16[16,5,24,512]{3,2,1,0:T(8,128)(2,1)S(1)} %get-tuple-element.5), channel_id=1, replica_groups={{9,7,13,11,10,5,2,0,15,14,4,3,6,12,1,8},{25,23,29,27,26,21,18,16,31,30,..., dimensions={0} | all-to-all | bytes 3932160 | tf_op jit(solution)/shard_map/all_to_all | solution.py:38
  33.0 0.0 copy-start.1
  33.0 1.0 %transform.1 = bf16[16,168,128]{2,1,0:T(8,128)(2,1)S(1)} custom-call(bf16[16,5,24,512]{3,2,1,0:T(8,128)(2,1)S(1)} %all_to_all.15.x_ref, bf16[128,384]{1,0:T(8,128)(2,1)S(1)} %get-tuple-element.6.m_ref, f32[4,128]{1,0:T(4,128)S(1)} %get-tuple-element.7.r_ref), custom_call_target="tpu_custom_call" | custom-call | tf_op jit(solution)/shard_map/transform/pallas_call | solution.py:155
  34.0 0.0 copy-start
  34.0 16.1 %all_to_all.16.y_ref = bf16[16,168,128]{2,1,0:T(8,128)(2,1)S(1)} all-to-all(bf16[16,168,128]{2,1,0:T(8,128)(2,1)S(1)} %transform.1), channel_id=1, replica_groups={{9,7,13,11,10,5,2,0,15,14,4,3,6,12,1,8},{25,23,29,27,26,21,18,16,31,30,..., dimensions={0} | all-to-all | bytes 1376256 | tf_op jit(solution)/shard_map/all_to_all | solution.py:38
  50.2 0.6 broadcast_in_dim.19
  50.8 11.5 %all-to-all-start.2 = ((f32[16,1,128]{2,1,0:T(1,128)}), f32[16,1,128]{2,1,0:T(1,128)S(1)}, u32[]{:S(2)}, u32[]{:S(2)}) async-start(f32[16,1,128]{2,1,0:T(1,128)} %broadcast_in_dim.19), calls=%async_computation.2 | async-start | bytes 16384 | tf_op jit(solution)/shard_map/all_to_all | solution.py:38
  62.3 0.0 copy-done.1
  62.3 1.8 %unpack.1 = f32[20,128,128]{2,1,0:T(8,128)} custom-call(bf16[16,168,128]{2,1,0:T(8,128)(2,1)S(1)} %all_to_all.16.y_ref), custom_call_target="tpu_custom_call" | custom-call | tf_op jit(solution)/shard_map/unpack/pallas_call | solution.py:178
  64.1 0.3 all-to-all-done.2
  64.4 0.0 copy-done
  64.4 0.8 %fusion.1 = f32[2,2,2,2]{3,2,1,0:T(2,128)} fusion(f32[2,2,2,2]{3,2,1,0:T(2,128)S(1)} %copy-done, f32[128]{0:T(128)S(1)} %reduce_sum.28, s32[2,2,2,2]{3,2,1,0:T(2,128)S(1)} %add_bitcast_fusion), kind=kLoop, calls=%fused_computation.3 | loop fusion | flops 8176 | bytes 704 | tf_op jit(solution)/shard_map/reduce_sum | solution.py:196
  (3 shorter events, 0.1 us)
Async XLA Ops:
  33.0 29.3 %copy-start.1 = (s32[2,2,2,2,1]{3,2,1,0,4:T(2,128)S(1)}, s32[2,2,2,2,1]{3,2,1,0,4:T(2,128)}, u32[]{:S(2)}) copy-start(s32[2,2,2,2,1]{3,2,1,0,4:T(2,128)} %constant.26.clone) | copy-start | bytes 196
  34.0 30.4 %copy-start = (f32[2,2,2,2]{3,2,1,0:T(2,128)S(1)}, f32[2,2,2,2]{3,2,1,0:T(2,128)}, u32[]{:S(2)}) copy-start(f32[2,2,2,2]{3,2,1,0:T(2,128)} %constant.29) | copy-start | bytes 196
  50.8 13.6 %all-to-all-start.2 = ((f32[16,1,128]{2,1,0:T(1,128)}), f32[16,1,128]{2,1,0:T(1,128)S(1)}, u32[]{:S(2)}, u32[]{:S(2)}) async-start(f32[16,1,128]{2,1,0:T(1,128)} %broadcast_in_dim.19), calls=%async_computation.2 | async-start | bytes 16384 | tf_op jit(solution)/shard_map/all_to_all | solution.py:38

commit v5 on v4

--- a/solution.py
+++ b/solution.py
@@ -2,12 +2,10 @@
 
 import jax
 import jax.numpy as jnp
-import numpy as np
 from jax import lax
 from jax.experimental import pallas as pl
 from jax.experimental.pallas import tpu as pltpu
 from jax.sharding import PartitionSpec as P
-
 
 VARS = 5
 BLK = 256
@@ -18,8 +16,8 @@
 LANES = 128
 VMEM_LIMIT = 16 << 20
 EXTRA = 8
-SPREAD = (9, 7, 13, 11, 10, 5, 2, 0, 15, 14, 4, 3, 6, 12, 1, 8)
-COLLECT = (9, 7, 13, 11, 10, 5, 2, 0, 15, 14, 4, 3, 6, 12, 1, 8)
+SPREAD = (11, 10, 0, 15, 12, 14, 8, 4, 7, 5, 1, 2, 13, 3, 9, 6)
+COLLECT = (14, 7, 8, 11, 10, 5, 2, 0, 15, 9, 4, 3, 6, 12, 1, 13)
 POINTS = (12, 0, 1, 2, 3, 4, 5, 6, 7, 8, 9, 10, 11, 13, 14, 15)
 
 
@@ -36,6 +34,17 @@
 def exchange(pieces, axes, order):
     groups = [list(order)] if len(order) == pieces.shape[0] else None
     return lax.all_to_all(pieces, axes, split_axis=0, concat_axis=0, tiled=True, axis_index_groups=groups)
+
+
+def cos_sin(turns):
+    quarter = ((turns + 32) >> 6) & 3
+    x = (((turns + 32) & 63) - 32).astype(jnp.float32) * jnp.float32(2.0 * math.pi / BLK)
+    y = x * x
+    cos = 1.0 + y * (-1 / 2 + y * (1 / 24 + y * (-1 / 720 + y * (1 / 40320 - y * (1 / 3628800)))))
+    sin = x * (1.0 + y * (-1 / 6 + y * (1 / 120 + y * (-1 / 5040 + y * (1 / 362880)))))
+    odd = (quarter & 1) == 1
+    cos, sin = jnp.where(odd, sin, cos), jnp.where(odd, cos, sin)
+    return jnp.where((quarter == 1) | (quarter == 2), -cos, cos), jnp.where(quarter >= 2, -sin, sin)
 
 
 def multipliers_of(index_ref, own):
@@ -46,10 +55,10 @@
     index = jnp.zeros((modes, BLK), jnp.int32)
     for f in range(modes):
         index = jnp.where(row == f % own * places + slots(COLLECT)[f // own], index_ref[f], index)
-    window = 0.5 - 0.5 * jnp.cos(2.0 * math.pi * lag.astype(jnp.float32) / BLK)
-    window = window / jnp.sqrt(jnp.float32(3.0 * BLK / 8.0))
-    angles = 2.0 * math.pi * ((index * lag) & (BLK - 1)).astype(jnp.float32) / BLK
-    return jnp.cos(angles) * window, -jnp.sin(angles) * window
+    window = 0.5 - 0.5 * cos_sin(lax.broadcasted_iota(jnp.int32, (8, BLK), 1))[0]
+    window = (window / jnp.sqrt(jnp.float32(3.0 * BLK / 8.0)))[:1]
+    cos, sin = cos_sin((index * lag) & (BLK - 1))
+    return cos * window, -sin * window
 
 
 def pack(shard, indices, weights, places, groups):
@@ -108,7 +117,7 @@
 
 
 def transform(gathered, multipliers, roots):
-    groups, variables, _, piece = gathered.shape
+    groups, variables, times, piece = gathered.shape
     tiles = piece // LANES
     modes = RETAINED_MODES
     own = modes // groups
@@ -166,34 +175,77 @@
     )(gathered, multipliers, roots)
 
 
-def unpack(received, rows, inner):
+def unpack(received, rows, inner, copies):
     groups, _, lanes = received.shape
     outer = rows // inner
-    per_step = 5
-
-    def body(y_ref, o_ref):
-        for s in range(groups):
-            o_ref[:, s * inner : (s + 1) * inner, :] = y_ref[slots(COLLECT)[s]].astype(jnp.float32).reshape(per_step, inner, lanes)
-
-    return pl.pallas_call(
-        body,
-        grid=(outer // per_step,),
-        in_specs=[pl.BlockSpec((groups, per_step * inner, lanes), lambda k: (0, k, 0))],
-        out_specs=pl.BlockSpec((per_step, groups * inner, lanes), lambda k: (k, 0, 0)),
-        out_shape=jax.ShapeDtypeStruct((outer, groups * inner, lanes), jnp.float32),
+
+    def body(y_ref, o_ref, sums_ref):
+        total = jnp.zeros((EXTRA, lanes), jnp.float32)
+        for s, place in enumerate(slots(COLLECT)):
+            piece = y_ref[place].astype(jnp.float32)
+            o_ref[:, s * inner : (s + 1) * inner, :] = piece[:rows].reshape(outer, inner, lanes)
+            total = total + piece[rows:]
+        sums_ref[...] = jnp.broadcast_to((total[:1] + total[1:2])[None], sums_ref.shape)
+
+    vmem = pl.BlockSpec(memory_space=pltpu.VMEM)
+    return pl.pallas_call(
+        body,
+        in_specs=[vmem],
+        out_specs=(vmem, vmem),
+        out_shape=(
+            pltpu.VMEM((outer, groups * inner, lanes), jnp.float32),
+            pltpu.VMEM((copies, 1, lanes), jnp.float32),
+        ),
         compiler_params=pltpu.CompilerParams(vmem_limit_bytes=VMEM_LIMIT),
         name="unpack",
     )(received)
 
 
-def gram_of(sums, slot, own, terms):
-    shape = (own, SEGMENT_NUMBER, SEGMENT_NUMBER, 2, 1)
-    f, b, b2, part, _ = np.indices(shape)
-    first = (np.where(b == b2, b, 2 + part) * own + f) * (RETAINED_MODES // own)
-    factor = np.where(part == 0, 1.0, b2 - b) / terms
-    lane = lax.broadcasted_iota(jnp.int32, shape[:4] + (LANES,), 4)
-    chosen = jnp.where(lane == jnp.asarray(first, jnp.int32) + slot, sums, 0.0)
-    return jnp.sum(chosen * jnp.asarray(factor, jnp.float32), axis=-1)
+def finish(spectra, sums, slot, groups, terms):
+    own = RETAINED_MODES // groups
+    entries = own * SEGMENT_NUMBER * SEGMENT_NUMBER
+    lanes = sums.shape[-1]
+    chunks = 4
+    size = spectra.shape[0] // chunks
+
+    def body(slot_ref, sums_ref, s_ref, o_hbm, gram_ref, sem):
+        copies = []
+        for k in range(chunks):
+            part = pl.ds(k * size, size)
+            copies.append(pltpu.make_async_copy(s_ref.at[part], o_hbm.at[part], sem.at[k]))
+            copies[-1].start()
+        total = sums_ref[0]
+        for k in range(1, sums_ref.shape[0]):
+            total = total + sums_ref[k]
+        row = lax.broadcasted_iota(jnp.int32, (entries, lanes), 0)
+        lane = lax.broadcasted_iota(jnp.int32, (entries, lanes), 1)
+        f, b, b2 = row >> 2, (row >> 1) & 1, row & 1
+
+        def chosen(q):
+            there = lane == (q * own + f) * groups + slot_ref[0]
+            return jnp.sum(jnp.where(there, total, 0.0), axis=1, keepdims=True) * jnp.float32(1.0 / terms)
+
+        real = chosen(jnp.where(b == b2, b, 2))
+        imag = chosen(3) * (b2 - b).astype(jnp.float32)
+        both = jnp.where(lane == 0, real, imag)
+        for k in range(entries // 2):
+            gram_ref[k] = both[2 * k : 2 * k + 2, :2]
+        for copy in copies:
+            copy.wait()
+
+    vmem = pl.BlockSpec(memory_space=pltpu.VMEM)
+    return pl.pallas_call(
+        body,
+        in_specs=[pl.BlockSpec(memory_space=pltpu.SMEM), vmem, vmem],
+        out_specs=(pl.BlockSpec(memory_space=pltpu.HBM), vmem),
+        out_shape=(
+            jax.ShapeDtypeStruct(spectra.shape, spectra.dtype),
+            jax.ShapeDtypeStruct((entries // 2, 2, 2), jnp.float32),
+        ),
+        scratch_shapes=[pltpu.SemaphoreType.DMA((chunks,))],
+        compiler_params=pltpu.CompilerParams(vmem_limit_bytes=VMEM_LIMIT),
+        name="finish",
+    )(slot, sums, spectra)
 
 
 def on_device(snapshots, quad_weights, spectral_indices):
@@ -208,19 +260,19 @@
     slot = slot_of(me, COLLECT)
     places = (me * groups + slot)[None]
     packed, multipliers, roots = pack(jnp.transpose(snapshots, (1, 0, 2)), spectral_indices, weights, places, groups)
-    gathered = exchange(packed, "ta", SPREAD)
+    with jax.named_scope("spread"):
+        gathered = exchange(packed, "ta", SPREAD)
     payload = transform(gathered, multipliers, roots)
-    received = exchange(payload, "ta", COLLECT)
+    with jax.named_scope("collect"):
+        received = exchange(payload, "ta", COLLECT)
 
     split = ("px", "py")
     copies = lax.axis_size(split)
-    sums = jnp.sum(received[:, rows : rows + 2].astype(jnp.float32), axis=(0, 1))
-    sums = jnp.broadcast_to(sums, (copies, 1, LANES))
-    sums = jnp.sum(exchange(sums, split, POINTS), axis=0)
-    terms = point_count * copies * VARS
-    gram = gram_of(sums, slot, own, terms)
-
-    spectra = unpack(received, rows, tiles * 2)
+    spectra, sums = unpack(received, rows, tiles * 2, copies)
+    with jax.named_scope("points"):
+        sums = exchange(sums, split, POINTS)
+    spectra, gram = finish(spectra, sums, slot[None], groups, point_count * copies * VARS)
+    gram = gram.reshape(own, SEGMENT_NUMBER, SEGMENT_NUMBER, 2)
     spectra = spectra.reshape(own, SEGMENT_NUMBER, VARS, point_count // LANES, 2, LANES)
     spectra = jnp.transpose(spectra, (0, 1, 4, 2, 3, 5)).reshape(own, SEGMENT_NUMBER, 2, VARS, point_count)
     return (spectra, gram)

time: 65.4 us -> 64.6 us (0.988)
  blocking collectives: 46.8 us -> 59.2 us
  starting transfers between devices: 11.5 us -> 0 us
  other arithmetic: 0.83 us -> 0 us
    all_to_all x2 -> x3, blocking collectives: 46.8 us -> 59.2 us  [exchange(): lax.all_to_all(pieces, axes, split_axis=0, concat_axis=0, tiled=True, axi...]
    all_to_all x1 -> x0, starting transfers between devices: 11.5 us -> none  [exchange(): lax.all_to_all(pieces, axes, split_axis=0, concat_axis=0, tiled=True, axi...]
    reduce_sum x3 -> x0, other arithmetic: 0.82 us -> none  [the longest x1 0.77 us: gram_of(): return jnp.sum(chosen * jnp.asarray(factor, jnp.float32), axis=-1)]
    pallas_call x1 -> x2, Pallas kernels: 1.76 us -> 1.82 us  [the longest x1 1.68 us: finish(): pl.pallas_call(body, in_specs=[pl.BlockSpec(memory_space=pltpu.SMEM), vme...]
  transfers between devices with their start and end apart: 1 -> 0, of which waited for: 1 -> 0; matrix products, arithmetic and copies ran while one was open for 0% -> 0% of each run, Pallas kernels for 3% -> 0%
where the time goes in v5:
time: 64.6 us; the launch traced here: 64.4 us
  blocking collectives  59.2 us (92%)
  Pallas kernels  4.53 us (7%)
  between operations  0.67 us (1%)
    all_to_all x3, blocking collectives, exchange(): lax.all_to_all(pieces, axes, split_axis=0, concat_axis=0, tiled=True, axi...  59.2 us
    pallas_call x1, Pallas kernels, pack(): pl.pallas_call(body, in_specs=[smem, hbm, hbm, hbm], out_specs=(vmem, vme...  1.76 us
    pallas_call x1, Pallas kernels, finish(): pl.pallas_call(body, in_specs=[pl.BlockSpec(memory_space=pltpu.SMEM), vme...  1.68 us

profile of v5, /device:TPU:1, one launch (start us, length us, event | category | flops | bytes accessed | tf_op | source)
XLA Modules:
  0.0 64.4 jit_solution(3714057772449015087)
XLA Ops:
  0.7 1.8 %pack.1 = (bf16[16,5,24,512]{3,2,1,0:T(8,128)(2,1)S(1)}, bf16[128,384]{1,0:T(8,128)(2,1)S(1)}, f32[4,128]{1,0:T(4,128)S(1)}) custom-call(s32[1]{0:T(128)} %bitcast.1.places_ref, s32[32]{0:T(128)} %index_hbm.1, f32[64,128]{1,0:T(8,128)} %bitcast.11, bf16[5,24,8192]{2,1,0:T(8,128)(2,1)} %bitcast.10), custom_call_target="tpu_custom_call" | custom-call | tf_op jit(solution)/shard_map/pack/pallas_call | solution.py:98
  2.4 30.7 %all_to_all.15.x_ref = bf16[16,5,24,512]{3,2,1,0:T(8,128)(2,1)S(1)} all-to-all(bf16[16,5,24,512]{3,2,1,0:T(8,128)(2,1)S(1)} %get-tuple-element.9), channel_id=1, replica_groups={{11,10,0,15,12,14,8,4,7,5,1,2,13,3,9,6},{27,26,16,31,28,30,24,20,23,21,..., dimensions={0} | all-to-all | bytes 3932160 | tf_op jit(solution)/shard_map/spread/all_to_all | solution.py:36
  33.1 1.0 %transform.1 = bf16[16,168,128]{2,1,0:T(8,128)(2,1)S(1)} custom-call(bf16[16,5,24,512]{3,2,1,0:T(8,128)(2,1)S(1)} %all_to_all.15.x_ref, bf16[128,384]{1,0:T(8,128)(2,1)S(1)} %get-tuple-element.10.m_ref, f32[4,128]{1,0:T(4,128)S(1)} %get-tuple-element.11.r_ref), custom_call_target="tpu_custom_call" | custom-call | tf_op jit(solution)/shard_map/transform/pallas_call | solution.py:164
  34.0 13.6 %all_to_all.16.y_ref = bf16[16,168,128]{2,1,0:T(8,128)(2,1)S(1)} all-to-all(bf16[16,168,128]{2,1,0:T(8,128)(2,1)S(1)} %transform.1), channel_id=1, replica_groups={{14,7,8,11,10,5,2,0,15,9,4,3,6,12,1,13},{30,23,24,27,26,21,18,16,31,25,..., dimensions={0} | all-to-all | bytes 1376256 | tf_op jit(solution)/shard_map/collect/all_to_all | solution.py:36
  47.7 0.1 unpack.1
  47.8 14.9 %all_to_all.17.sums_ref = f32[16,1,128]{2,1,0:T(1,128)S(1)} all-to-all(f32[16,1,128]{2,1,0:T(1,128)S(1)} %get-tuple-element.12), channel_id=1, replica_groups={{192,0,16,32,48,64,80,96,112,128,144,160,176,208,224,240},{193,1,17,33,..., dimensions={0} | all-to-all | bytes 16384 | tf_op jit(solution)/shard_map/points/all_to_all | solution.py:36
  62.7 1.7 %finish.1 = (f32[20,128,128]{2,1,0:T(8,128)}, f32[4,2,2]{2,1,0:T(2,128)}) custom-call(s32[1]{0:T(128)} %bitcast.slot_ref, f32[16,1,128]{2,1,0:T(1,128)S(1)} %all_to_all.17.sums_ref, f32[20,128,128]{2,1,0:T(8,128)S(1)} %get-tuple-element.13.s_ref), custom_call_target="tpu_custom_call" | custom-call | tf_op jit(solution)/shard_map/finish/pallas_call | solution.py:237

commit v6 on v5

--- a/solution.py
+++ b/solution.py
@@ -16,8 +16,8 @@
 LANES = 128
 VMEM_LIMIT = 16 << 20
 EXTRA = 8
-SPREAD = (11, 10, 0, 15, 12, 14, 8, 4, 7, 5, 1, 2, 13, 3, 9, 6)
-COLLECT = (14, 7, 8, 11, 10, 5, 2, 0, 15, 9, 4, 3, 6, 12, 1, 13)
+SPREAD = (11, 10, 4, 15, 12, 14, 8, 0, 7, 5, 1, 2, 13, 3, 9, 6)
+COLLECT = (14, 7, 2, 11, 10, 13, 3, 15, 1, 9, 5, 0, 6, 12, 8, 4)
 POINTS = (12, 0, 1, 2, 3, 4, 5, 6, 7, 8, 9, 10, 11, 13, 14, 15)
 
 
@@ -68,14 +68,11 @@
 
     tiles = piece // LANES
 
-    def body(places_ref, index_hbm, w_hbm, x_hbm, o_ref, m_ref, r_ref, index_ref, w_ref, sem, index_sem, w_sem):
+    def body(places_ref, index_hbm, w_hbm, x_hbm, o_ref, m_ref, r_ref, index_ref, w_ref, x_ref, sem, index_sem, w_sem):
         get_index = pltpu.make_async_copy(index_hbm, index_ref, index_sem)
         get_weights = pltpu.make_async_copy(w_hbm, w_ref, w_sem)
         get_index.start()
-        copies = [
-            pltpu.make_async_copy(x_hbm.at[:, :, pl.ds(d * piece, piece)], o_ref.at[slots(SPREAD)[d]], sem.at[d])
-            for d in range(groups)
-        ]
+        copies = [pltpu.make_async_copy(x_hbm.at[v], x_ref.at[v], sem.at[v]) for v in range(variables)]
         for copy in copies:
             copy.start()
         get_weights.start()
@@ -88,8 +85,10 @@
         get_weights.wait()
         me = lax.div(places_ref[0], groups)
         r_ref[...] = jnp.sqrt(w_ref[pl.ds(me * tiles, tiles), :])
-        for copy in copies:
+        for v, copy in enumerate(copies):
             copy.wait()
+            for d, slot in enumerate(slots(SPREAD)):
+                o_ref[slot, v] = x_ref[v, :, d * piece : (d + 1) * piece]
 
     vmem = pl.BlockSpec(memory_space=pltpu.VMEM)
     smem = pl.BlockSpec(memory_space=pltpu.SMEM)
@@ -107,7 +106,8 @@
         scratch_shapes=[
             pltpu.SMEM(indices.shape, indices.dtype),
             pltpu.VMEM(weights.shape, weights.dtype),
-            pltpu.SemaphoreType.DMA((groups,)),
+            pltpu.VMEM(shard.shape, shard.dtype),
+            pltpu.SemaphoreType.DMA((variables,)),
             pltpu.SemaphoreType.DMA,
             pltpu.SemaphoreType.DMA,
         ],

time: 64.6 us -> 64.2 us (level)
  no operation moved by 1% of the time
where the time goes in v6:
time: 64.2 us; the launch traced here: 64 us
  blocking collectives  59 us (92%)
  Pallas kernels  4.33 us (7%)
  between operations  0.67 us (1%)
    all_to_all x3, blocking collectives, exchange(): lax.all_to_all(pieces, axes, split_axis=0, concat_axis=0, tiled=True, axi...  59 us
    pallas_call x1, Pallas kernels, finish(): pl.pallas_call(body, in_specs=[pl.BlockSpec(memory_space=pltpu.SMEM), vme...  1.68 us
    pallas_call x1, Pallas kernels, pack(): pl.pallas_call(body, in_specs=[smem, hbm, hbm, hbm], out_specs=(vmem, vme...  1.56 us

profile of v6, /device:TPU:1, one launch (start us, length us, event | category | flops | bytes accessed | tf_op | source)
XLA Modules:
  0.0 64.0 jit_solution(13838053660587785409)
XLA Ops:
  0.7 1.6 %pack.1 = (bf16[16,5,24,512]{3,2,1,0:T(8,128)(2,1)S(1)}, bf16[128,384]{1,0:T(8,128)(2,1)S(1)}, f32[4,128]{1,0:T(4,128)S(1)}) custom-call(s32[1]{0:T(128)} %bitcast.1.places_ref, s32[32]{0:T(128)} %index_hbm.1, f32[64,128]{1,0:T(8,128)} %bitcast.11, bf16[5,24,8192]{2,1,0:T(8,128)(2,1)} %bitcast.10), custom_call_target="tpu_custom_call" | custom-call | tf_op jit(solution)/shard_map/pack/pallas_call | solution.py:97
  2.2 30.9 %all_to_all.15.x_ref = bf16[16,5,24,512]{3,2,1,0:T(8,128)(2,1)S(1)} all-to-all(bf16[16,5,24,512]{3,2,1,0:T(8,128)(2,1)S(1)} %get-tuple-element.9), channel_id=1, replica_groups={{11,10,4,15,12,14,8,0,7,5,1,2,13,3,9,6},{27,26,20,31,28,30,24,16,23,21,..., dimensions={0} | all-to-all | bytes 3932160 | tf_op jit(solution)/shard_map/spread/all_to_all | solution.py:36
  33.1 1.0 %transform.1 = bf16[16,168,128]{2,1,0:T(8,128)(2,1)S(1)} custom-call(bf16[16,5,24,512]{3,2,1,0:T(8,128)(2,1)S(1)} %all_to_all.15.x_ref, bf16[128,384]{1,0:T(8,128)(2,1)S(1)} %get-tuple-element.10.m_ref, f32[4,128]{1,0:T(4,128)S(1)} %get-tuple-element.11.r_ref), custom_call_target="tpu_custom_call" | custom-call | tf_op jit(solution)/shard_map/transform/pallas_call | solution.py:164
  34.1 14.2 %all_to_all.16.y_ref = bf16[16,168,128]{2,1,0:T(8,128)(2,1)S(1)} all-to-all(bf16[16,168,128]{2,1,0:T(8,128)(2,1)S(1)} %transform.1), channel_id=1, replica_groups={{14,7,2,11,10,13,3,15,1,9,5,0,6,12,8,4},{30,23,18,27,26,29,19,31,17,25,..., dimensions={0} | all-to-all | bytes 1376256 | tf_op jit(solution)/shard_map/collect/all_to_all | solution.py:36
  48.3 0.1 unpack.1
  48.4 13.9 %all_to_all.17.sums_ref = f32[16,1,128]{2,1,0:T(1,128)S(1)} all-to-all(f32[16,1,128]{2,1,0:T(1,128)S(1)} %get-tuple-element.12), channel_id=1, replica_groups={{192,0,16,32,48,64,80,96,112,128,144,160,176,208,224,240},{193,1,17,33,..., dimensions={0} | all-to-all | bytes 16384 | tf_op jit(solution)/shard_map/points/all_to_all | solution.py:36
  62.3 1.7 %finish.1 = (f32[20,128,128]{2,1,0:T(8,128)}, f32[4,2,2]{2,1,0:T(2,128)}) custom-call(s32[1]{0:T(128)} %bitcast.slot_ref, f32[16,1,128]{2,1,0:T(1,128)S(1)} %all_to_all.17.sums_ref, f32[20,128,128]{2,1,0:T(8,128)S(1)} %get-tuple-element.13.s_ref), custom_call_target="tpu_custom_call" | custom-call | tf_op jit(solution)/shard_map/finish/pallas_call | solution.py:237

commit v7 on v6

--- a/solution.py
+++ b/solution.py
@@ -201,19 +201,12 @@
     )(received)
 
 
-def finish(spectra, sums, slot, groups, terms):
+def gram_of(sums, slot, groups, terms):
     own = RETAINED_MODES // groups
     entries = own * SEGMENT_NUMBER * SEGMENT_NUMBER
     lanes = sums.shape[-1]
-    chunks = 4
-    size = spectra.shape[0] // chunks
-
-    def body(slot_ref, sums_ref, s_ref, o_hbm, gram_ref, sem):
-        copies = []
-        for k in range(chunks):
-            part = pl.ds(k * size, size)
-            copies.append(pltpu.make_async_copy(s_ref.at[part], o_hbm.at[part], sem.at[k]))
-            copies[-1].start()
+
+    def body(slot_ref, sums_ref, gram_ref):
         total = sums_ref[0]
         for k in range(1, sums_ref.shape[0]):
             total = total + sums_ref[k]
@@ -230,22 +223,16 @@
         both = jnp.where(lane == 0, real, imag)
         for k in range(entries // 2):
             gram_ref[k] = both[2 * k : 2 * k + 2, :2]
-        for copy in copies:
-            copy.wait()
-
-    vmem = pl.BlockSpec(memory_space=pltpu.VMEM)
-    return pl.pallas_call(
-        body,
-        in_specs=[pl.BlockSpec(memory_space=pltpu.SMEM), vmem, vmem],
-        out_specs=(pl.BlockSpec(memory_space=pltpu.HBM), vmem),
-        out_shape=(
-            jax.ShapeDtypeStruct(spectra.shape, spectra.dtype),
-            jax.ShapeDtypeStruct((entries // 2, 2, 2), jnp.float32),
-        ),
-        scratch_shapes=[pltpu.SemaphoreType.DMA((chunks,))],
-        compiler_params=pltpu.CompilerParams(vmem_limit_bytes=VMEM_LIMIT),
-        name="finish",
-    )(slot, sums, spectra)
+
+    vmem = pl.BlockSpec(memory_space=pltpu.VMEM)
+    return pl.pallas_call(
+        body,
+        in_specs=[pl.BlockSpec(memory_space=pltpu.SMEM), vmem],
+        out_specs=vmem,
+        out_shape=jax.ShapeDtypeStruct((entries // 2, 2, 2), jnp.float32),
+        compiler_params=pltpu.CompilerParams(vmem_limit_bytes=VMEM_LIMIT),
+        name="gram",
+    )(slot, sums)
 
 
 def on_device(snapshots, quad_weights, spectral_indices):
@@ -271,7 +258,7 @@
     spectra, sums = unpack(received, rows, tiles * 2, copies)
     with jax.named_scope("points"):
         sums = exchange(sums, split, POINTS)
-    spectra, gram = finish(spectra, sums, slot[None], groups, point_count * copies * VARS)
+    gram = gram_of(sums, slot[None], groups, point_count * copies * VARS)
     gram = gram.reshape(own, SEGMENT_NUMBER, SEGMENT_NUMBER, 2)
     spectra = spectra.reshape(own, SEGMENT_NUMBER, VARS, point_count // LANES, 2, LANES)
     spectra = jnp.transpose(spectra, (0, 1, 4, 2, 3, 5)).reshape(own, SEGMENT_NUMBER, 2, VARS, point_count)

time: 64.2 us -> 63.9 us (level)
  blocking collectives: 59 us -> 45.1 us
  starting transfers between devices: 0 us -> 12 us
  local copies, waits for them, and re-layouts: 0 us -> 1.06 us
  waiting for transfers between devices: 0 us -> 1.02 us
    all_to_all x3 -> x2, blocking collectives: 59 us -> 45.1 us  [exchange(): lax.all_to_all(pieces, axes, split_axis=0, concat_axis=0, tiled=True, axi...]
    all_to_all x0 -> x1, starting transfers between devices: none -> 12 us  [exchange(): lax.all_to_all(pieces, axes, split_axis=0, concat_axis=0, tiled=True, axi...]
    unnamed x0 -> x1, local copies, waits for them, and re-layouts: none -> 1.06 us
    all_to_all x0 -> x1, waiting for transfers between devices: none -> 1.02 us  [exchange(): lax.all_to_all(pieces, axes, split_axis=0, concat_axis=0, tiled=True, axi...]
    pallas_call x1, Pallas kernels: 1.68 us -> 0.69 us  [gram_of(): pl.pallas_call(body, in_specs=[pl.BlockSpec(memory_space=pltpu.SMEM), vme...]
  transfers between devices with their start and end apart: 0 -> 1, of which waited for: 0 -> 1; matrix products, arithmetic and copies ran while one was open for 0% -> 2% of each run, Pallas kernels for 0% -> 0%
where the time goes in v7:
time: 63.9 us; the launch traced here: 63.7 us
  blocking collectives  45.1 us (71%)
  starting transfers between devices  12 us (19%)
  Pallas kernels  3.89 us (6%)
  local copies, waits for them, and re-layouts  1.06 us (2%)
  waiting for transfers between devices  1.02 us (2%)
  between operations  0.66 us (1%)
    all_to_all x2, blocking collectives, exchange(): lax.all_to_all(pieces, axes, split_axis=0, concat_axis=0, tiled=True, axi...  45.1 us
    all_to_all x1, starting transfers between devices, exchange(): lax.all_to_all(pieces, axes, split_axis=0, concat_axis=0, tiled=True, axi...  12 us
    pallas_call x1, Pallas kernels, pack(): pl.pallas_call(body, in_specs=[smem, hbm, hbm, hbm], out_specs=(vmem, vme...  1.56 us
  transfers between devices with their start and end apart: 1, of which 1 were waited for; matrix products, arithmetic and copies ran while one was open for 2% of the time, Pallas kernels for 0%

profile of v7, /device:TPU:1, one launch (start us, length us, event | category | flops | bytes accessed | tf_op | source)
XLA Modules:
  0.0 63.7 jit_solution(6141126078758355167)
XLA Ops:
  0.7 1.6 %pack.1 = (bf16[16,5,24,512]{3,2,1,0:T(8,128)(2,1)S(1)}, bf16[128,384]{1,0:T(8,128)(2,1)S(1)}, f32[4,128]{1,0:T(4,128)S(1)}) custom-call(s32[1]{0:T(128)} %bitcast.places_ref, s32[32]{0:T(128)} %index_hbm.1, f32[64,128]{1,0:T(8,128)} %bitcast.12, bf16[5,24,8192]{2,1,0:T(8,128)(2,1)} %bitcast.11), custom_call_target="tpu_custom_call" | custom-call | tf_op jit(solution)/shard_map/pack/pallas_call | solution.py:97
  2.2 30.9 %all_to_all.15.x_ref = bf16[16,5,24,512]{3,2,1,0:T(8,128)(2,1)S(1)} all-to-all(bf16[16,5,24,512]{3,2,1,0:T(8,128)(2,1)S(1)} %get-tuple-element.7), channel_id=1, replica_groups={{11,10,4,15,12,14,8,0,7,5,1,2,13,3,9,6},{27,26,20,31,28,30,24,16,23,21,..., dimensions={0} | all-to-all | bytes 3932160 | tf_op jit(solution)/shard_map/spread/all_to_all | solution.py:36
  33.1 1.0 %transform.1 = bf16[16,168,128]{2,1,0:T(8,128)(2,1)S(1)} custom-call(bf16[16,5,24,512]{3,2,1,0:T(8,128)(2,1)S(1)} %all_to_all.15.x_ref, bf16[128,384]{1,0:T(8,128)(2,1)S(1)} %get-tuple-element.8.m_ref, f32[4,128]{1,0:T(4,128)S(1)} %get-tuple-element.9.r_ref), custom_call_target="tpu_custom_call" | custom-call | tf_op jit(solution)/shard_map/transform/pallas_call | solution.py:164
  34.1 14.2 %all_to_all.16.y_ref = bf16[16,168,128]{2,1,0:T(8,128)(2,1)S(1)} all-to-all(bf16[16,168,128]{2,1,0:T(8,128)(2,1)S(1)} %transform.1), channel_id=1, replica_groups={{14,7,2,11,10,13,3,15,1,9,5,0,6,12,8,4},{30,23,18,27,26,29,19,31,17,25,..., dimensions={0} | all-to-all | bytes 1376256 | tf_op jit(solution)/shard_map/collect/all_to_all | solution.py:36
  48.3 0.7 %unpack.1 = (f32[20,128,128]{2,1,0:T(8,128)S(1)}, f32[16,1,128]{2,1,0:T(1,128)}) custom-call(bf16[16,168,128]{2,1,0:T(8,128)(2,1)S(1)} %all_to_all.16.y_ref), custom_call_target="tpu_custom_call" | custom-call | tf_op jit(solution)/shard_map/unpack/pallas_call | solution.py:191
  48.9 12.0 %all-to-all-start.2 = ((f32[16,1,128]{2,1,0:T(1,128)}), f32[16,1,128]{2,1,0:T(1,128)S(1)}, u32[]{:S(2)}, u32[]{:S(2)}) async-start(f32[16,1,128]{2,1,0:T(1,128)} %get-tuple-element.11), calls=%async_computation.2 | async-start | bytes 16384 | tf_op jit(solution)/shard_map/points/all_to_all | solution.py:36
  60.9 1.1 %copy.9 = f32[2,2,2,5,8192]{4,2,3,1,0:T(2,128)} copy(f32[2,2,2,5,8192]{4,2,3,1,0:T(2,128)S(1)} %bitcast.10) | data formatting | bytes 2621440
  62.0 1.0 %all-to-all-done.2.sums_ref = f32[16,1,128]{2,1,0:T(1,128)S(1)} async-done(((f32[16,1,128]{2,1,0:T(1,128)}), f32[16,1,128]{2,1,0:T(1,128)S(1)}, u32[]{:S(2)}, u32[]{:S(2)}) %all-to-all-start.2) | async-done | bytes 8224 | tf_op jit(solution)/shard_map/points/all_to_all | solution.py:36
  63.0 0.7 %gram.1 = f32[4,2,2]{2,1,0:T(2,128)} custom-call(s32[1]{0:T(128)} %bitcast.6.slot_ref, f32[16,1,128]{2,1,0:T(1,128)S(1)} %all-to-all-done.2.sums_ref), custom_call_target="tpu_custom_call" | custom-call | tf_op jit(solution)/shard_map/gram/pallas_call | solution.py:228
Async XLA Ops:
  48.9 14.1 %all-to-all-start.2 = ((f32[16,1,128]{2,1,0:T(1,128)}), f32[16,1,128]{2,1,0:T(1,128)S(1)}, u32[]{:S(2)}, u32[]{:S(2)}) async-start(f32[16,1,128]{2,1,0:T(1,128)} %get-tuple-element.11), calls=%async_computation.2 | async-start | bytes 16384 | tf_op jit(solution)/shard_map/points/all_to_all | solution.py:36

commit v8 on v7

--- a/solution.py
+++ b/solution.py
@@ -179,23 +179,28 @@
     groups, _, lanes = received.shape
     outer = rows // inner
 
-    def body(y_ref, o_ref, sums_ref):
+    def body(y_ref, o_ref, sums_hbm, sums_ref, sem):
         total = jnp.zeros((EXTRA, lanes), jnp.float32)
+        for place in range(groups):
+            total = total + y_ref[place, rows:, :].astype(jnp.float32)
+        sums_ref[...] = jnp.broadcast_to((total[:1] + total[1:2])[None], sums_ref.shape)
+        copy = pltpu.make_async_copy(sums_ref, sums_hbm, sem)
+        copy.start()
         for s, place in enumerate(slots(COLLECT)):
-            piece = y_ref[place].astype(jnp.float32)
-            o_ref[:, s * inner : (s + 1) * inner, :] = piece[:rows].reshape(outer, inner, lanes)
-            total = total + piece[rows:]
-        sums_ref[...] = jnp.broadcast_to((total[:1] + total[1:2])[None], sums_ref.shape)
+            piece = y_ref[place, :rows, :].astype(jnp.float32)
+            o_ref[:, s * inner : (s + 1) * inner, :] = piece.reshape(outer, inner, lanes)
+        copy.wait()
 
     vmem = pl.BlockSpec(memory_space=pltpu.VMEM)
     return pl.pallas_call(
         body,
         in_specs=[vmem],
-        out_specs=(vmem, vmem),
+        out_specs=(vmem, pl.BlockSpec(memory_space=pltpu.HBM)),
         out_shape=(
             pltpu.VMEM((outer, groups * inner, lanes), jnp.float32),
-            pltpu.VMEM((copies, 1, lanes), jnp.float32),
+            jax.ShapeDtypeStruct((copies, 1, lanes), jnp.float32),
         ),
+        scratch_shapes=[pltpu.VMEM((copies, 1, lanes), jnp.float32), pltpu.SemaphoreType.DMA],
         compiler_params=pltpu.CompilerParams(vmem_limit_bytes=VMEM_LIMIT),
         name="unpack",
     )(received)

time: 63.9 us -> 63.9 us (level)
  no operation moved by 1% of the time
where the time goes in v8:
time: 63.9 us; the launch traced here: 63.7 us
  blocking collectives  45.1 us (71%)
  starting transfers between devices  12 us (19%)
  Pallas kernels  3.86 us (6%)
  local copies, waits for them, and re-layouts  1.06 us (2%)
  waiting for transfers between devices  1.02 us (2%)
  between operations  0.67 us (1%)
    all_to_all x2, blocking collectives, exchange(): lax.all_to_all(pieces, axes, split_axis=0, concat_axis=0, tiled=True, axi...  45.1 us
    all_to_all x1, starting transfers between devices, exchange(): lax.all_to_all(pieces, axes, split_axis=0, concat_axis=0, tiled=True, axi...  12 us
    pallas_call x1, Pallas kernels, pack(): pl.pallas_call(body, in_specs=[smem, hbm, hbm, hbm], out_specs=(vmem, vme...  1.56 us
  transfers between devices with their start and end apart: 1, of which 1 were waited for; matrix products, arithmetic and copies ran while one was open for 2% of the time, Pallas kernels for 0%

profile of v8, /device:TPU:1, one launch (start us, length us, event | category | flops | bytes accessed | tf_op | source)
XLA Modules:
  0.0 63.7 jit_solution(652919899072857205)
XLA Ops:
  0.7 1.6 %pack.1 = (bf16[16,5,24,512]{3,2,1,0:T(8,128)(2,1)S(1)}, bf16[128,384]{1,0:T(8,128)(2,1)S(1)}, f32[4,128]{1,0:T(4,128)S(1)}) custom-call(s32[1]{0:T(128)} %bitcast.places_ref, s32[32]{0:T(128)} %index_hbm.1, f32[64,128]{1,0:T(8,128)} %bitcast.12, bf16[5,24,8192]{2,1,0:T(8,128)(2,1)} %bitcast.11), custom_call_target="tpu_custom_call" | custom-call | tf_op jit(solution)/shard_map/pack/pallas_call | solution.py:97
  2.2 30.9 %all_to_all.15.x_ref = bf16[16,5,24,512]{3,2,1,0:T(8,128)(2,1)S(1)} all-to-all(bf16[16,5,24,512]{3,2,1,0:T(8,128)(2,1)S(1)} %get-tuple-element.7), channel_id=1, replica_groups={{11,10,4,15,12,14,8,0,7,5,1,2,13,3,9,6},{27,26,20,31,28,30,24,16,23,21,..., dimensions={0} | all-to-all | bytes 3932160 | tf_op jit(solution)/shard_map/spread/all_to_all | solution.py:36
  33.1 1.0 %transform.1 = bf16[16,168,128]{2,1,0:T(8,128)(2,1)S(1)} custom-call(bf16[16,5,24,512]{3,2,1,0:T(8,128)(2,1)S(1)} %all_to_all.15.x_ref, bf16[128,384]{1,0:T(8,128)(2,1)S(1)} %get-tuple-element.8.m_ref, f32[4,128]{1,0:T(4,128)S(1)} %get-tuple-element.9.r_ref), custom_call_target="tpu_custom_call" | custom-call | tf_op jit(solution)/shard_map/transform/pallas_call | solution.py:164
  34.1 14.2 %all_to_all.16.y_ref = bf16[16,168,128]{2,1,0:T(8,128)(2,1)S(1)} all-to-all(bf16[16,168,128]{2,1,0:T(8,128)(2,1)S(1)} %transform.1), channel_id=1, replica_groups={{14,7,2,11,10,13,3,15,1,9,5,0,6,12,8,4},{30,23,18,27,26,29,19,31,17,25,..., dimensions={0} | all-to-all | bytes 1376256 | tf_op jit(solution)/shard_map/collect/all_to_all | solution.py:36
  48.3 0.7 %unpack.1 = (f32[20,128,128]{2,1,0:T(8,128)S(1)}, f32[16,1,128]{2,1,0:T(1,128)}) custom-call(bf16[16,168,128]{2,1,0:T(8,128)(2,1)S(1)} %all_to_all.16.y_ref), custom_call_target="tpu_custom_call" | custom-call | tf_op jit(solution)/shard_map/unpack/pallas_call | solution.py:195
  48.9 12.0 %all-to-all-start.2 = ((f32[16,1,128]{2,1,0:T(1,128)}), f32[16,1,128]{2,1,0:T(1,128)S(1)}, u32[]{:S(2)}, u32[]{:S(2)}) async-start(f32[16,1,128]{2,1,0:T(1,128)} %get-tuple-element.11), calls=%async_computation.2 | async-start | bytes 16384 | tf_op jit(solution)/shard_map/points/all_to_all | solution.py:36
  60.9 1.1 %copy.9 = f32[2,2,2,5,8192]{4,2,3,1,0:T(2,128)} copy(f32[2,2,2,5,8192]{4,2,3,1,0:T(2,128)S(1)} %bitcast.10) | data formatting | bytes 2621440
  62.0 1.0 %all-to-all-done.2.sums_ref = f32[16,1,128]{2,1,0:T(1,128)S(1)} async-done(((f32[16,1,128]{2,1,0:T(1,128)}), f32[16,1,128]{2,1,0:T(1,128)S(1)}, u32[]{:S(2)}, u32[]{:S(2)}) %all-to-all-start.2) | async-done | bytes 8224 | tf_op jit(solution)/shard_map/points/all_to_all | solution.py:36
  63.0 0.7 %gram.1 = f32[4,2,2]{2,1,0:T(2,128)} custom-call(s32[1]{0:T(128)} %bitcast.6.slot_ref, f32[16,1,128]{2,1,0:T(1,128)S(1)} %all-to-all-done.2.sums_ref), custom_call_target="tpu_custom_call" | custom-call | tf_op jit(solution)/shard_map/gram/pallas_call | solution.py:233
Async XLA Ops:
  48.9 14.1 %all-to-all-start.2 = ((f32[16,1,128]{2,1,0:T(1,128)}), f32[16,1,128]{2,1,0:T(1,128)S(1)}, u32[]{:S(2)}, u32[]{:S(2)}) async-start(f32[16,1,128]{2,1,0:T(1,128)} %get-tuple-element.11), calls=%async_computation.2 | async-start | bytes 16384 | tf_op jit(solution)/shard_map/points/all_to_all | solution.py:36
